TPU v7x, 128 devices: a whole 4x4x4 slice. The times are simulated.
128 devices in a mesh: sim: 32 (over z, y, x_hi), learn: 4 (over x_lo, core).
Axes of the slice: x: 4 (x_hi: 2, x_lo: 2; x = x_hi * 2 + x_lo), y: 4, z: 4, core: 2. Of those that a mesh axis runs over, the one named last changes fastest.
Arguments:
- state_field: float32 [128, 512, 2048], P(None, 'sim', 'learn'), may hold values from -6 to 6
- diffusion: float32 [128], replicated, may hold values from 0.03 to 0.24
- weight_in: float32 [128, 1024], replicated, may hold values from -0.5 to 0.5
- weight_mid: float32 [1024, 1024], replicated, may hold values from -0.1875 to 0.1875
- weight_out: float32 [1024, 128], replicated, may hold values from -0.1875 to 0.1875
- block_tile: int32 [1536, 1], P('learn'), may hold values from 0 to 31; in each aligned block of 12 rows (0 to 11, 12 to 23, ...) no two rows name the same one
- block_pos: int32 [1536], P('learn'), may hold values from 0 to 63
Outputs:
- new_state: float32 [128, 512, 2048], P(None, 'sim', 'learn')
- new_in: float32 [128, 1024], replicated
- new_mid: float32 [1024, 1024], replicated
- new_out: float32 [1024, 128], replicated
Inputs may be any that keep to these rules, and one draw needn't show every extreme that they name: `block_tile`: in each aligned block of 12 rows no tile index appears twice.
All inputs are finite; a program needn't handle non-finite values.
Results may differ from a plain program's by a relative error of at most 0.0003.
The roundings to bfloat16 on the way count: a program that leaves them out, or rounds other values in their place, can miss the bound.
Values may be sent and summed in bfloat16 or wider, within the bound.
No kernel may reach another device: no remote copies, remote signals or barrier semaphores. Data moves between devices by JAX's collectives and lax.ppermute only.
A program may use at most 128 MiB of HBM per device.

v0:
```python
import jax
import jax.numpy as jnp
from jax import lax
from jax.sharding import PartitionSpec as P

BW = 128


RATE = 0.5
TARGET_GAIN = 4.0


def with_halo(x, sides, width):
    for axis, dim in sides:
        size, length = (lax.axis_size(axis), x.shape[dim])
        up = [(i, (i + 1) % size) for i in range(size)]
        down = [(j, i) for i, j in up]
        last = lax.slice_in_dim(x, length - width, length, axis=dim)
        first = lax.slice_in_dim(x, 0, width, axis=dim)
        before = lax.ppermute(last, axis, up)
        after = lax.ppermute(first, axis, down)
        x = jnp.concatenate([before, x, after], axis=dim)
    return x


def interior_step(padded, diffusion):
    center = padded[:, 1:-1, 1:-1]
    beside_all = padded[:, :-2, 1:-1] + padded[:, 2:, 1:-1]
    beside_all = beside_all + padded[:, 1:-1, :-2] + padded[:, 1:-1, 2:]
    return center + diffusion[:, None, None] * (beside_all - 4.0 * center)


def silu_slope(value):
    sigma = jax.nn.sigmoid(value)
    return sigma * (1.0 + value * (1.0 - sigma))


def gradients(inputs, targets, weight_in, weight_mid, weight_out, count):
    first = weight_in.astype(jnp.bfloat16)
    second = weight_mid.astype(jnp.bfloat16)
    third = weight_out.astype(jnp.bfloat16)
    pre_one = jnp.dot(inputs, first, preferred_element_type=jnp.float32)
    act_one = jax.nn.silu(pre_one).astype(jnp.bfloat16)
    pre_two = jnp.dot(act_one, second, preferred_element_type=jnp.float32)
    act_two = jax.nn.silu(pre_two).astype(jnp.bfloat16)
    output = jnp.dot(act_two, third, preferred_element_type=jnp.float32)
    error = ((output - targets.astype(jnp.float32)) / count).astype(jnp.bfloat16)
    grad_out = jnp.dot(act_two.T, error, preferred_element_type=jnp.float32)
    back_two = jnp.dot(error, third.T, preferred_element_type=jnp.float32)
    delta_two = (back_two * silu_slope(pre_two)).astype(jnp.bfloat16)
    grad_mid = jnp.dot(act_one.T, delta_two, preferred_element_type=jnp.float32)
    back_one = jnp.dot(delta_two, second.T, preferred_element_type=jnp.float32)
    delta_one = (back_one * silu_slope(pre_one)).astype(jnp.bfloat16)
    grad_in = jnp.dot(inputs.T, delta_one, preferred_element_type=jnp.float32)
    return (grad_in, grad_mid, grad_out)


def on_device(state_field, diffusion, weight_in, weight_mid, weight_out, block_tile, block_pos):
    levels, tile_rows, tile_cols = state_field.shape
    padded = with_halo(state_field, (("sim", 1), ("learn", 2)), 2)
    after = interior_step(interior_step(padded, diffusion), diffusion)
    increment = after - state_field
    senders = lax.axis_size("sim")
    own_index = lax.axis_index("sim")
    samples = block_tile.shape[0] // senders
    per_row = tile_cols // BW
    tiles = block_tile[:, 0].reshape(senders, samples)
    places = block_pos.reshape(senders, samples)
    matched = tiles == own_index
    place = jnp.sum(jnp.where(matched, places, 0), axis=1)
    present = jnp.any(matched, axis=1)

    def cut(spot):
        row = spot // per_row
        start = spot % per_row * BW
        zero = jnp.zeros((), jnp.int32)
        piece_in = lax.dynamic_slice(state_field, (zero, row, start), (levels, 1, BW))[:, 0, :]
        piece_target = lax.dynamic_slice(increment, (zero, row, start), (levels, 1, BW))[:, 0, :]
        return (piece_in, piece_target)

    cols_in, cols_target = jax.vmap(cut)(place)
    keep = present[:, None, None]
    send_in = jnp.where(keep, jnp.swapaxes(cols_in, 1, 2), 0.0).astype(jnp.bfloat16)
    send_target = jnp.where(keep, TARGET_GAIN * jnp.swapaxes(cols_target, 1, 2), 0.0).astype(
        jnp.bfloat16
    )
    got_in, got_target = (
        lax.all_to_all(send_in, "sim", split_axis=0, concat_axis=0, tiled=True),
        lax.all_to_all(send_target, "sim", split_axis=0, concat_axis=0, tiled=True),
    )
    wanted = lax.dynamic_slice_in_dim(tiles, own_index, 1, 0)[0]
    inputs = jnp.take(got_in, wanted, axis=0).reshape(-1, levels)
    targets = jnp.take(got_target, wanted, axis=0).reshape(-1, levels)
    count = float(senders * lax.axis_size("learn") * samples * BW)
    grad_in, grad_mid, grad_out = gradients(
        inputs, targets, weight_in, weight_mid, weight_out, count
    )
    total_in, total_mid, total_out = lax.psum((grad_in, grad_mid, grad_out), ("sim", "learn"))
    new_in = weight_in - RATE * total_in
    new_mid = weight_mid - RATE * total_mid
    new_out = weight_out - RATE * total_out
    return (after, new_in, new_mid, new_out)


def solution(mesh):
    placed = (P(None, "sim", "learn"), P(), P(), P(), P(), P("learn", None), P("learn"))
    return jax.shard_map(
        on_device,
        mesh=mesh,
        in_specs=placed,
        out_specs=(P(None, "sim", "learn"), P(), P(), P()),
        check_vma=False,
    )
```

profile of v0, /device:TPU:1, one launch (start us, length us, event | category | flops | bytes accessed | tf_op | source)
XLA Modules:
  0.0 309.2 jit_solution(2728969360066584125)
XLA Ops:
  7.2 5.8 %copy.26 = f32[128,16,512]{0,1,2:T(8,128)} copy(f32[128,16,512]{2,1,0:T(8,128)} %param.9) | data formatting | bytes 8388608 | tf_op args[0]
  13.0 2.6 fusion.34
  15.6 3.6 %collective-permute-start = (f32[128,2,512]{0,1,2:T(2,128)S(1)}, f32[128,2,512]{0,1,2:T(2,128)S(1)}, u32[]{:S(2)}, u32[]{:S(2)}) collective-permute-start(f32[128,2,512]{0,1,2:T(2,128)S(1)} %get-tuple-element.28), channel_id=1, source_target_pairs={{0,4},{4,8},{8,12},{12,16},{16,20},{20,24},{24,28},{28,32},{32,36}... | collective-permute-start | bytes 1572872 | tf_op jit(solution)/shard_map/ppermute | solution.py:20
  19.2 6.0 %collective-permute-start.1 = (f32[128,2,512]{0,1,2:T(2,128)S(1)}, f32[128,2,512]{0,1,2:T(2,128)S(1)}, u32[]{:S(2)}, u32[]{:S(2)}) collective-permute-start(f32[128,2,512]{0,1,2:T(2,128)S(1)} %get-tuple-element.29), channel_id=1, source_target_pairs={{4,0},{8,4},{12,8},{16,12},{20,16},{24,20},{28,24},{32,28},{36,32}... | collective-permute-start | bytes 1572872 | tf_op jit(solution)/shard_map/ppermute | solution.py:21
  25.7 6.2 %gather_fusion = bf16[32,128,128]{1,0,2:T(8,128)(2,1)S(1)} fusion(f32[128,16,512]{0,1,2:T(8,128)} %copy.26, s32[32]{0:T(128)S(1)} %fusion.28), kind=kCustom, calls=%fused_computation.2 | custom fusion | bytes 2097536 | tf_op jit(solution)/shard_map/vmap()/gather | solution.py:77
  31.9 4.9 %collective-permute-done = f32[128,2,512]{0,1,2:T(2,128)S(1)} collective-permute-done((f32[128,2,512]{0,1,2:T(2,128)S(1)}, f32[128,2,512]{0,1,2:T(2,128)S(1)}, u32[]{:S(2)}, u32[]{:S(2)}) %collective-permute-start) | collective-permute-done | bytes 524320 | tf_op jit(solution)/shard_map/ppermute | solution.py:20
  36.8 6.3 %collective-permute-done.1 = f32[128,2,512]{0,1,2:T(2,128)S(1)} collective-permute-done((f32[128,2,512]{0,1,2:T(2,128)S(1)}, f32[128,2,512]{0,1,2:T(2,128)S(1)}, u32[]{:S(2)}, u32[]{:S(2)}) %collective-permute-start.1) | collective-permute-done | bytes 524320 | tf_op jit(solution)/shard_map/ppermute | solution.py:21
  43.8 2.7 collective-permute-start.2
  48.1 10.2 %all-to-all-start = ((bf16[32,128,128]{2,1,0:T(8,128)(2,1)}), bf16[32,128,128]{2,1,0:T(8,128)(2,1)}, u32[]{:S(2)}, u32[]{:S(2)}) async-start(bf16[32,128,128]{2,1,0:T(8,128)(2,1)} %copy.30), calls=%async_computation | async-start | bytes 2097152 | tf_op jit(solution)/shard_map/all_to_all | solution.py:88
  58.4 4.3 %pad_maximum_fusion = f32[128,20,516]{0,1,2:T(8,128)S(1)} fusion(f32[128,20,2]{0,1,2:T(8,128)S(1)} %collective-permute-done.3, f32[128,2,512]{0,1,2:T(2,128)S(1)} %collective-permute-done.1, f32[128,16,512]{0,1,2:T(8,128)} %copy.26, f32[128,2,512]{0,1,2:T(2,128)S(1)} %collective-permute-done, f32[128,20,2]{0,1,2:T(8,128)S(1)} %collective-permute-done.2), kind=kLoop, calls=%fused_computation.4 | loop fusion | flops 5283840 | bytes 10567680 | tf_op jit(solution)/shard_map/concatenate | solution.py:22
  62.7 7.1 %fusion.3 = f32[128,18,514]{0,1,2:T(8,128)S(1)} fusion(f32[128,20,2]{0,1,2:T(8,128)S(1)} %collective-permute-done.3, f32[128,2,512]{0,1,2:T(2,128)S(1)} %collective-permute-done.1, f32[128,16,512]{0,1,2:T(8,128)S(1)} %copy-done, f32[128,2,512]{0,1,2:T(2,128)S(1)} %collective-permute-done, f32[128,20,2]{0,1,2:T(8,128)S(1)} %collective-permute-done.2, ...), kind=kLoop, calls=%fused_computation.9 | loop fusion | flops 15395328 | bytes 24232448 | tf_op jit(solution)/shard_map/add | solution.py:30
  69.8 4.7 %fusion.31 = (f32[128,16,512]{0,1,2:T(8,128)}, f32[128,16,512]{0,1,2:T(8,128)}) fusion(f32[128,16,512]{0,1,2:T(8,128)S(1)} %copy-done, f32[128,18,514]{0,1,2:T(8,128)S(1)} %fusion.3, f32[128]{0:T(128)S(1)} %copy-done.8), kind=kLoop, calls=%fused_computation.75 | loop fusion | flops 8388608 | bytes 33554944 | tf_op jit(solution)/shard_map/sub | solution.py:62
  74.5 6.1 %gather_fusion.1 = f32[32,128,128]{1,0,2:T(8,128)S(1)} fusion(f32[128,16,512]{0,1,2:T(8,128)} %get-tuple-element.20, s32[32]{0:T(128)S(1)} %fusion.28), kind=kCustom, calls=%fused_computation.3 | custom fusion | bytes 4194688 | tf_op jit(solution)/shard_map/vmap()/gather | solution.py:78
  82.4 9.1 %all-to-all-start.1 = ((bf16[32,128,128]{2,1,0:T(8,128)(2,1)}), bf16[32,128,128]{2,1,0:T(8,128)(2,1)S(1)}, u32[]{:S(2)}, u32[]{:S(2)}) async-start(bf16[32,128,128]{2,1,0:T(8,128)(2,1)} %copy.32), calls=%async_computation.1 | async-start | bytes 2097152 | tf_op jit(solution)/shard_map/all_to_all | solution.py:89
  91.8 1.8 gather_fusion.2
  93.7 15.7 %all-to-all-done.1 = bf16[32,128,128]{2,1,0:T(8,128)(2,1)S(1)} async-done(((bf16[32,128,128]{2,1,0:T(8,128)(2,1)}), bf16[32,128,128]{2,1,0:T(8,128)(2,1)S(1)}, u32[]{:S(2)}, u32[]{:S(2)}) %all-to-all-start.1) | async-done | bytes 1048608 | tf_op jit(solution)/shard_map/all_to_all | solution.py:89
  112.3 4.5 %multiply_convert_fusion.2 = (bf16[1536,1024]{1,0:T(8,128)(2,1)S(1)}, f32[1536,1024]{1,0:T(8,128)S(1)}) fusion(f32[1024,1024]{1,0:T(8,128)S(1)} %copy-done.2, f32[1536,1024]{1,0:T(8,128)S(1)} %fusion.18), kind=kOutput, calls=%fused_computation.19 | convolution fusion | flops 3238002688 | bytes 19922944 | tf_op jit(solution)/shard_map/dot_general | solution.py:44
  117.8 1.8 fusion.35
  119.6 2.7 multiply_convert_fusion.1
  124.0 5.1 %fusion.30 = f32[1024,1024]{1,0:T(8,128)} fusion(bf16[1536,1024]{1,0:T(8,128)(2,1)S(1)} %multiply_convert_fusion.1, f32[1536,1024]{1,0:T(8,128)S(1)} %fusion.18), kind=kOutput, calls=%fused_computation.74 | convolution fusion | flops 3229089792 | bytes 13631488 | tf_op jit(solution)/shard_map/dot_general | solution.py:51
  129.1 10.6 %fusion.11 = f32[128,1024]{1,0:T(8,128)} fusion(bf16[1536,128]{1,0:T(8,128)(2,1)S(1)} %bitcast.36, f32[1536,1024]{1,0:T(8,128)} %copy-done.1, bf16[1536,1024]{1,0:T(8,128)(2,1)} %copy-done.10, f32[1024,1024]{1,0:T(8,128)} %param.12), kind=kOutput, calls=%fused_computation.36 | convolution fusion | flops 3639083008 | bytes 14548992 | tf_op jit(solution)/shard_map/dot_general | solution.py:54
  139.7 5.6 %copy.33 = f32[128,16,512]{2,1,0:T(8,128)} copy(f32[128,16,512]{0,1,2:T(8,128)} %get-tuple-element.21) | data formatting | bytes 8388608
  145.2 148.4 %all-reduce.3.cloned.1.call-done = (f32[128,1024]{1,0:T(8,128)}, f32[1024,1024]{1,0:T(8,128)}, f32[1024,128]{1,0:T(8,128)}) async-done(((f32[128,1024]{1,0:T(8,128)}, f32[1024,1024]{1,0:T(8,128)}, f32[1024,128]{1,0:T(8,128)}), (f32[128,1024]{1,0:T(8,128)}, f32[1024,1024]{1,0:T(8,128)}, f32[1024,128]{1,0:T(8,128)})) %all-reduce.3.cloned.1.call-update) | async-done | bytes 5242896 | tf_op jit(solution)/shard_map/psum | solution.py:98
  293.7 7.0 %multiply_subtract_fusion = f32[1024,1024]{1,0:T(8,128)} fusion(f32[1024,1024]{1,0:T(8,128)} %param.12, f32[1024,1024]{1,0:T(8,128)} %get-tuple-element.18), kind=kLoop, calls=%fused_computation.29 | loop fusion | flops 2097152 | bytes 12582912 | tf_op jit(solution)/shard_map/sub | solution.py:100
  (47 shorter events, 12.1 us)
Async XLA Ops:
  7.2 18.1 %copy-start.9 = (s32[384,1]{0,1:T(1,128)S(1)}, s32[384,1]{0,1:T(1,128)}, u32[]{:S(2)}) copy-start(s32[384,1]{0,1:T(1,128)} %param.14) | copy-start | bytes 4612
  7.2 18.2 %copy-start.7 = (s32[384]{0:T(512)S(1)}, s32[384]{0:T(512)}, u32[]{:S(2)}) copy-start(s32[384]{0:T(512)} %param.15) | copy-start | bytes 4612
  15.6 21.2 %collective-permute-start = (f32[128,2,512]{0,1,2:T(2,128)S(1)}, f32[128,2,512]{0,1,2:T(2,128)S(1)}, u32[]{:S(2)}, u32[]{:S(2)}) collective-permute-start(f32[128,2,512]{0,1,2:T(2,128)S(1)} %get-tuple-element.28), channel_id=1, source_target_pairs={{0,4},{4,8},{8,12},{12,16},{16,20},{20,24},{24,28},{28,32},{32,36}... | collective-permute-start | bytes 1572872 | tf_op jit(solution)/shard_map/ppermute | solution.py:20
  19.2 23.8 %collective-permute-start.1 = (f32[128,2,512]{0,1,2:T(2,128)S(1)}, f32[128,2,512]{0,1,2:T(2,128)S(1)}, u32[]{:S(2)}, u32[]{:S(2)}) collective-permute-start(f32[128,2,512]{0,1,2:T(2,128)S(1)} %get-tuple-element.29), channel_id=1, source_target_pairs={{4,0},{8,4},{12,8},{16,12},{20,16},{24,20},{28,24},{32,28},{36,32}... | collective-permute-start | bytes 1572872 | tf_op jit(solution)/shard_map/ppermute | solution.py:21
  43.8 14.6 %collective-permute-start.2 = (f32[128,20,2]{0,1,2:T(8,128)S(1)}, f32[128,20,2]{0,1,2:T(8,128)S(1)}, u32[]{:S(2)}, u32[]{:S(2)}) collective-permute-start(f32[128,20,2]{0,1,2:T(8,128)S(1)} %get-tuple-element.26), channel_id=1, source_target_pairs={{0,1},{1,2},{2,3},{3,0},{4,5},{5,6},{6,7},{7,4},{8,9},{9,10},{10,1... | collective-permute-start | bytes 61448 | tf_op jit(solution)/shard_map/ppermute | solution.py:20
  46.5 11.9 %collective-permute-start.3 = (f32[128,20,2]{0,1,2:T(8,128)S(1)}, f32[128,20,2]{0,1,2:T(8,128)S(1)}, u32[]{:S(2)}, u32[]{:S(2)}) collective-permute-start(f32[128,20,2]{0,1,2:T(8,128)S(1)} %get-tuple-element.27), channel_id=1, source_target_pairs={{1,0},{2,1},{3,2},{0,3},{5,4},{6,5},{7,6},{4,7},{9,8},{10,9},{11,1... | collective-permute-start | bytes 61448 | tf_op jit(solution)/shard_map/ppermute | solution.py:21
  48.1 34.3 %all-to-all-start = ((bf16[32,128,128]{2,1,0:T(8,128)(2,1)}), bf16[32,128,128]{2,1,0:T(8,128)(2,1)}, u32[]{:S(2)}, u32[]{:S(2)}) async-start(bf16[32,128,128]{2,1,0:T(8,128)(2,1)} %copy.30), calls=%async_computation | async-start | bytes 2097152 | tf_op jit(solution)/shard_map/all_to_all | solution.py:88
  58.4 4.3 %copy-start = (f32[128,16,512]{0,1,2:T(8,128)S(1)}, f32[128,16,512]{0,1,2:T(8,128)}, u32[]{:S(2)}) copy-start(f32[128,16,512]{0,1,2:T(8,128)} %copy.26) | copy-start | bytes 12582916
  58.4 4.3 %copy-start.8 = (f32[128]{0:T(128)S(1)}, f32[128]{0:T(128)}, u32[]{:S(2)}) copy-start(f32[128]{0:T(128)} %param.10) | copy-start | bytes 1540
  80.6 29.6 %copy-start.4 = (f32[128,1024]{1,0:T(8,128)S(1)}, f32[128,1024]{1,0:T(8,128)}, u32[]{:S(2)}) copy-start(f32[128,1024]{1,0:T(8,128)} %param.11) | copy-start | bytes 1572868
  82.4 27.0 %all-to-all-start.1 = ((bf16[32,128,128]{2,1,0:T(8,128)(2,1)}), bf16[32,128,128]{2,1,0:T(8,128)(2,1)S(1)}, u32[]{:S(2)}, u32[]{:S(2)}) async-start(bf16[32,128,128]{2,1,0:T(8,128)(2,1)} %copy.32), calls=%async_computation.1 | async-start | bytes 2097152 | tf_op jit(solution)/shard_map/all_to_all | solution.py:89
  91.5 202.1 %all-reduce.3.cloned.1.call-start = ((), (), s32[]{:S(2)}) async-start(), calls=%async_computation.2 | async-start | bytes 10485760 | tf_op jit(solution)/shard_map/psum | solution.py:98
  110.1 2.2 copy-start.2
  112.3 10.1 %copy-start.1 = (f32[1536,1024]{1,0:T(8,128)}, f32[1536,1024]{1,0:T(8,128)S(1)}, u32[]{:S(2)}) copy-start(f32[1536,1024]{1,0:T(8,128)S(1)} %fusion.18) | copy-start | bytes 18874372
  112.3 4.5 %copy-start.3 = (f32[1024,128]{1,0:T(8,128)S(1)}, f32[1024,128]{1,0:T(8,128)}, u32[]{:S(2)}) copy-start(f32[1024,128]{1,0:T(8,128)} %param.13) | copy-start | bytes 1572868
  122.3 1.7 copy-start.10
  293.7 7.0 %copy-start.6 = (f32[1024,128]{1,0:T(8,128)S(1)}, f32[1024,128]{1,0:T(8,128)}, u32[]{:S(2)}) copy-start(f32[1024,128]{1,0:T(8,128)} %get-tuple-element.19) | copy-start | bytes 1572868
  293.7 7.8 %copy-start.5 = (f32[128,1024]{1,0:T(8,128)S(1)}, f32[128,1024]{1,0:T(8,128)}, u32[]{:S(2)}) copy-start(f32[128,1024]{1,0:T(8,128)} %get-tuple-element.17) | copy-start | bytes 1572868
Sparse Core Ops, SparseCore 0:
  139.8 153.7 all-reduce.2
where the time goes:
time: 310 us; the launch traced here: 309 us
  waiting for transfers between devices  175 us (56%)
  local copies, waits for them, and re-layouts  34.4 us (11%)
  starting transfers between devices  32 us (10%)
  matrix products  26.7 us (9%)
  other arithmetic  26.5 us (9%)
  between operations  14.3 us (5%)
    psum x1, waiting for transfers between devices, on_device(): lax.psum((grad_in, grad_mid, grad_out), ('sim', 'learn'))  148 us
    all_to_all x1, waiting for transfers between devices, on_device(): lax.all_to_all(send_target, 'sim', split_axis=0, concat_axis=0, tiled=True)  15.7 us
    unnamed x24, local copies, waits for them, and re-layouts  14.1 us
    dot_general x1, matrix products, gradients(): grad_in = jnp.dot(inputs.T, delta_one, preferred_element_type=jnp.float32)  10.6 us
    all_to_all x1, starting transfers between devices, on_device(): lax.all_to_all(send_in, 'sim', split_axis=0, concat_axis=0, tiled=True)  10.2 us
    all_to_all x1, starting transfers between devices, on_device(): lax.all_to_all(send_target, 'sim', split_axis=0, concat_axis=0, tiled=True)  9.14 us
    add x1, other arithmetic, interior_step(): return center + diffusion[:, None, None] * (beside_all - 4.0 * center)  7.08 us
    sub x1, other arithmetic, on_device(): new_mid = weight_mid - RATE * total_mid  6.98 us
  transfers between devices with their start and end apart: 7, of which 4 were waited for; matrix products, arithmetic and copies ran while one was open for 13% of the time, Pallas kernels for 0%

commit v1 on v0

v1 whole, which is shorter than its diff:
```python
import functools
import math

import jax
import jax.numpy as jnp
from jax import lax
from jax.experimental import pallas as pl
from jax.experimental.pallas import tpu as pltpu
from jax.sharding import Mesh
from jax.sharding import PartitionSpec as P

BW = 128
RATE = 0.5
TARGET_GAIN = 4.0
STEP = 4

SIM = ("z", "y", "xh")
LEARN = ("xl", "c")
RING = ("xh", "xl")
PLANE = ("z", "y")

BF16 = jnp.bfloat16
F32 = jnp.float32


def with_halo(x, sides, width):
    for axis, dim in sides:
        size, length = (lax.axis_size(axis), x.shape[dim])
        up = [(i, (i + 1) % size) for i in range(size)]
        down = [(j, i) for i, j in up]
        last = lax.slice_in_dim(x, length - width, length, axis=dim)
        first = lax.slice_in_dim(x, 0, width, axis=dim)
        before = lax.ppermute(last, axis, up)
        after = lax.ppermute(first, axis, down)
        x = jnp.concatenate([before, x, after], axis=dim)
    return x


def interior_step(padded, diffusion):
    center = padded[:, 1:-1, 1:-1]
    beside_all = padded[:, :-2, 1:-1] + padded[:, 2:, 1:-1]
    beside_all = beside_all + padded[:, 1:-1, :-2] + padded[:, 1:-1, 2:]
    return center + diffusion[:, None, None] * (beside_all - 4.0 * center)


def dot(a, b):
    return jnp.dot(a, b, preferred_element_type=F32)


def dot_t(a, b):
    return lax.dot_general(a, b, (((1,), (1,)), ((), ())), preferred_element_type=F32)


def activate(value):
    sigma = 0.5 * jnp.tanh(0.5 * value) + 0.5
    act = value * sigma
    return act.astype(BF16), sigma + act * (1.0 - sigma)


def network_kernel(
    count,
    meta,
    state,
    after,
    w1t,
    w2t,
    w2,
    w3t,
    w3,
    gin,
    gmid,
    gout,
    xbuf,
    abuf,
    slope1,
    slope2,
    sems,
):
    total = meta[0]
    steps = (total + STEP - 1) // STEP
    per_row = state.shape[2] // BW
    levels = w1t.shape[1]
    hid = w2.shape[0]

    def copies(step, slot, i):
        spot = meta[1 + step * STEP + i]
        row, col = spot // per_row, pl.multiple_of((spot % per_row) * BW, BW)
        lanes = pl.ds(i * BW, BW)
        return (
            pltpu.make_async_copy(
                state.at[:, row, pl.ds(col, BW)], xbuf.at[slot, :, lanes], sems.at[slot, i, 0]
            ),
            pltpu.make_async_copy(
                after.at[:, row, pl.ds(col, BW)], abuf.at[slot, :, lanes], sems.at[slot, i, 1]
            ),
        )

    def fetch(step, slot):
        for i in range(STEP):

            @pl.when(step * STEP + i < total)
            def _():
                for copy in copies(step, slot, i):
                    copy.start()

    gin[...] = jnp.zeros_like(gin)
    gmid[...] = jnp.zeros_like(gmid)
    gout[...] = jnp.zeros_like(gout)

    @pl.when(steps > 0)
    def _():
        fetch(0, 0)

    def body(step, carry):
        slot = lax.rem(step, 2)

        @pl.when(step + 1 < steps)
        def _():
            fetch(step + 1, 1 - slot)

        for i in range(STEP):
            index = step * STEP + i

            @pl.when(index < total)
            def _():
                for copy in copies(step, slot, i):
                    copy.wait()

            @pl.when(index >= total)
            def _():
                zero = jnp.zeros((levels, BW), F32)
                xbuf[slot, :, i * BW : (i + 1) * BW] = zero
                abuf[slot, :, i * BW : (i + 1) * BW] = zero

        x = xbuf[slot]
        inputs = x.astype(BF16)
        targets = (TARGET_GAIN * (abuf[slot] - x)).astype(BF16)
        act_one, slope1[...] = activate(dot(w1t[...], inputs))
        act_two, slope2[...] = activate(dot(w2t[...], act_one))
        output = dot(w3t[...], act_two)
        error = ((output - targets.astype(F32)) / count).astype(BF16)
        gout[...] += dot_t(act_two, error)
        delta_two = (dot(w3[...], error) * slope2[...]).astype(BF16)
        for j in range(0, hid, 2 * BW):
            both = dot_t(act_one, delta_two[j : j + 2 * BW])
            gmid[j // BW] += both[:, :BW]
            gmid[j // BW + 1] += both[:, BW:]
        delta_one = (dot(w2[...], delta_two) * slope1[...]).astype(BF16)
        for j in range(0, hid, 2 * BW):
            both = dot_t(inputs, delta_one[j : j + 2 * BW])
            gin[j // BW] += both[:, :BW]
            gin[j // BW + 1] += both[:, BW:]
        return carry

    lax.fori_loop(0, steps, body, 0)


def network(meta, state, after, weight_in, weight_mid, weight_out, count):
    levels, hid = weight_in.shape
    first, second, third = (w.astype(BF16) for w in (weight_in, weight_mid, weight_out))
    vmem = pl.BlockSpec(memory_space=pltpu.VMEM)
    hbm = pl.BlockSpec(memory_space=pl.ANY)
    width = STEP * BW
    return pl.pallas_call(
        functools.partial(network_kernel, count),
        out_shape=(
            jax.ShapeDtypeStruct((hid // BW, levels, BW), F32),
            jax.ShapeDtypeStruct((hid // BW, hid, BW), F32),
            jax.ShapeDtypeStruct((hid, levels), F32),
        ),
        in_specs=[pl.BlockSpec(memory_space=pltpu.SMEM), hbm, hbm] + [vmem] * 5,
        out_specs=(vmem, vmem, vmem),
        scratch_shapes=[
            pltpu.VMEM((2, levels, width), F32),
            pltpu.VMEM((2, levels, width), F32),
            pltpu.VMEM((hid, width), F32),
            pltpu.VMEM((hid, width), F32),
            pltpu.SemaphoreType.DMA((2, STEP, 2)),
        ],
        compiler_params=pltpu.CompilerParams(vmem_limit_bytes=56 * 1024 * 1024),
        name="network",
    )(meta, state, after, first.T, second.T, second, third.T, third)


def sum_everywhere(grad_in, grad_mid, grad_out):
    core = lax.axis_index("c")
    parts = [g.reshape(2, -1, BW) for g in (grad_in, grad_mid, grad_out)]
    other = [lax.dynamic_index_in_dim(g, 1 - core, 0, False) for g in parts]
    own = [lax.dynamic_index_in_dim(g, core, 0, False) for g in parts]

    def packed(g_in, g_mid, g_out):
        high = lax.reduce_precision(g_out, 8, 7)
        low = (g_out - high).astype(BF16)
        high = high.astype(BF16)
        return jnp.concatenate([g_in.astype(BF16), g_mid.astype(BF16), high, low])

    n_in, n_mid, n_out = (g.shape[0] for g in own)
    cut = (n_in, n_in + n_mid, n_in + n_mid + n_out)
    got = lax.ppermute(packed(*other), "c", [(0, 1), (1, 0)]).astype(F32)
    pair = packed(
        own[0] + got[: cut[0]],
        own[1] + got[cut[0] : cut[1]],
        own[2] + (got[cut[1] : cut[2]] + got[cut[2] :]),
    )
    ring, plane = lax.axis_size(RING), lax.axis_size(PLANE)
    held = lax.all_to_all(pair, RING, 0, 0, tiled=True)
    held = jnp.sum(held.reshape(ring, -1, BW).astype(F32), axis=0)
    held = lax.all_to_all(held, PLANE, 0, 0, tiled=True)
    held = jnp.sum(held.reshape(plane, -1, BW), axis=0)
    rows = held.shape[0]
    largest = jnp.max(jnp.abs(held))
    power = jnp.floor(jnp.log2(jnp.maximum(largest, 1e-30)))
    sent = (held * jnp.exp2(14.0 - power)).astype(jnp.float16)
    sent = jnp.concatenate([sent, jnp.full((8, BW), power, jnp.float16)])
    for axis, size in ((PLANE, plane), (RING, ring)):
        spread = jnp.broadcast_to(sent, (size,) + sent.shape).reshape(-1, BW)
        sent = lax.all_to_all(spread, axis, 0, 0, tiled=True)
    away = lax.ppermute(sent, "c", [(0, 1), (1, 0)])

    def opened(block):
        block = block.reshape(ring * plane, rows + 8, BW).astype(F32)
        scale = jnp.exp2(block[:, rows : rows + 1] - 14.0)
        return (block[:, :rows] * scale).reshape(-1, BW)

    mine, theirs = opened(sent), opened(away)
    low_half = jnp.where(core == 0, mine, theirs)
    high_half = jnp.where(core == 0, theirs, mine)
    halves = (low_half, high_half)
    total_in = jnp.concatenate([h[: cut[0]] for h in halves])
    total_mid = jnp.concatenate([h[cut[0] : cut[1]] for h in halves])
    total_out = jnp.concatenate([h[cut[1] : cut[2]] + h[cut[2] :] for h in halves])
    return total_in, total_mid, total_out


def on_device(state_field, diffusion, weight_in, weight_mid, weight_out, block_tile, block_pos):
    levels, tile_rows, tile_cols = state_field.shape
    padded = with_halo(state_field, ((SIM, 1), (LEARN, 2)), 2)
    after = interior_step(interior_step(padded, diffusion), diffusion)
    senders = lax.axis_size(SIM)
    own_index = lax.axis_index(SIM)
    samples = block_tile.shape[0] // senders
    tiles = block_tile[:, 0].reshape(senders, samples)
    places = block_pos.reshape(senders, samples)
    matched = tiles == own_index
    place = jnp.sum(jnp.where(matched, places, 0), axis=1)
    present = jnp.any(matched, axis=1)
    order = jnp.arange(senders)
    rank = jnp.sum(jnp.where(order[None, :] < order[:, None], present[None, :], False), axis=1)
    lands = present[:, None] & (rank[:, None] == order[None, :])
    slots = jnp.sum(jnp.where(lands, place[:, None], 0), axis=0)
    meta = jnp.concatenate([jnp.sum(present.astype(jnp.int32))[None], slots.astype(jnp.int32)])
    count = float(senders * lax.axis_size(LEARN) * samples * BW)
    grads = network(meta, state_field, after, weight_in, weight_mid, weight_out, count)
    total_in, total_mid, total_out = sum_everywhere(*grads)
    hid = weight_in.shape[1]
    total_in = jnp.swapaxes(total_in.reshape(hid // BW, levels, BW), 0, 1).reshape(levels, hid)
    total_mid = jnp.swapaxes(total_mid.reshape(hid // BW, hid, BW), 0, 1).reshape(hid, hid)
    new_in = weight_in - RATE * total_in
    new_mid = weight_mid - RATE * total_mid
    new_out = weight_out - RATE * total_out
    return (after, new_in, new_mid, new_out)


def solution(mesh):
    fine = Mesh(mesh.devices.reshape(4, 4, 2, 2, 2), SIM + LEARN)
    placed = (P(None, SIM, LEARN), P(), P(), P(), P(), P(LEARN, None), P(LEARN))
    return jax.shard_map(
        on_device,
        mesh=fine,
        in_specs=placed,
        out_specs=(P(None, SIM, LEARN), P(), P(), P()),
        check_vma=False,
    )
```

time: 310 us -> 231 us (0.75)
  waiting for transfers between devices: 175 us -> 22.2 us
  blocking collectives: 0 us -> 91.6 us
  matrix products: 26.7 us -> 0 us
  other arithmetic: 26.5 us -> 51.8 us
  Pallas kernels: 0 us -> 22.4 us
  starting transfers between devices: 32 us -> 17.3 us
  between operations: 14.3 us -> 1.69 us
  local copies, waits for them, and re-layouts: 34.4 us -> 22.4 us
    psum x1 -> x0, waiting for transfers between devices: 148 us -> none  [on_device(): lax.psum((grad_in, grad_mid, grad_out), ('sim', 'learn'))]
    all_to_all x0 -> x4, blocking collectives: none -> 91.6 us  [the longest x1 38.8 us: sum_everywhere(): held = lax.all_to_all(held, PLANE, 0, 0, tiled=True)]
    dot_general x7 -> x0, matrix products: 26.7 us -> none  [the longest x1 10.6 us: gradients(): grad_in = jnp.dot(inputs.T, delta_one, preferred_element_type=jnp.float32)]
    pallas_call x0 -> x1, Pallas kernels: none -> 22.4 us  [network(): pl.pallas_call(functools.partial(network_kernel, count), out_shape=(jax.S...]
    all_to_all x2 -> x0, starting transfers between devices: 19.4 us -> none  [the longest x1 10.2 us: on_device(): lax.all_to_all(send_in, 'sim', split_axis=0, concat_axis=0, tiled=True)]
    all_to_all x2 -> x0, waiting for transfers between devices: 15.7 us -> none  [the longest x1 15.7 us: on_device(): lax.all_to_all(send_target, 'sim', split_axis=0, concat_axis=0, tiled=True)]
    gather x4 -> x0, local copies, waits for them, and re-layouts: 14.7 us -> none  [the longest x1 6.16 us: cut(): lax.dynamic_slice(state_field, (zero, row, start), (levels, 1, BW))[:, 0, :]]
    add x1 -> x2, other arithmetic: 7.08 us -> 19.7 us  [interior_step(): return center + diffusion[:, None, None] * (beside_all - 4.0 * center)]
  transfers between devices with their start and end apart: 7 -> 6, of which waited for: 4 -> 4; matrix products, arithmetic and copies ran while one was open for 13% -> 9% of each run, Pallas kernels for 0% -> 0%
where the time goes in v1:
time: 231 us; the launch traced here: 229 us
  blocking collectives  91.6 us (40%)
  other arithmetic  51.8 us (22%)
  local copies, waits for them, and re-layouts  22.4 us (10%)
  Pallas kernels  22.4 us (10%)
  waiting for transfers between devices  22.2 us (10%)
  starting transfers between devices  17.3 us (7%)
    all_to_all x1, blocking collectives, sum_everywhere(): held = lax.all_to_all(held, PLANE, 0, 0, tiled=True)  38.8 us
    all_to_all x2, blocking collectives, sum_everywhere(): sent = lax.all_to_all(spread, axis, 0, 0, tiled=True)  30.3 us
    all_to_all x1, blocking collectives, sum_everywhere(): held = lax.all_to_all(pair, RING, 0, 0, tiled=True)  22.5 us
    pallas_call x1, Pallas kernels, network(): pl.pallas_call(functools.partial(network_kernel, count), out_shape=(jax.S...  22.4 us
    add x2, other arithmetic, interior_step(): return center + diffusion[:, None, None] * (beside_all - 4.0 * center)  19.7 us
    ppermute x2, waiting for transfers between devices, with_halo(): before = lax.ppermute(last, axis, up)  12.1 us
    ppermute x2, starting transfers between devices, with_halo(): after = lax.ppermute(first, axis, down)  11.1 us
    concatenate x1, other arithmetic, with_halo(): x = jnp.concatenate([before, x, after], axis=dim)  7.91 us
  transfers between devices with their start and end apart: 6, of which 4 were waited for; matrix products, arithmetic and copies ran while one was open for 9% of the time, Pallas kernels for 0%

profile of v1, /device:TPU:1, one launch (start us, length us, event | category | flops | bytes accessed | tf_op | source)
XLA Modules:
  0.0 229.5 jit_solution(3907921063676228401)
XLA Ops:
  0.6 3.7 %fusion.25 = (f32[128,2,512]{2,1,0:T(2,128)}, f32[128,2,512]{2,1,0:T(2,128)}) fusion(f32[128,16,512]{2,1,0:T(8,128)} %state.1), kind=kLoop, calls=%fused_computation.72 | loop fusion | bytes 2097152 | tf_op jit(solution)/shard_map/slice | solution.py:31
  4.3 9.5 %collective-permute-start.1 = (f32[128,2,512]{2,1,0:T(2,128)}, f32[128,2,512]{2,1,0:T(2,128)S(1)}, u32[]{:S(2)}, u32[]{:S(2)}) collective-permute-start(f32[128,2,512]{2,1,0:T(2,128)} %get-tuple-element.17), channel_id=1, source_target_pairs={{4,0},{8,4},{12,8},{16,12},{20,16},{24,20},{28,24},{32,28},{36,32}... | collective-permute-start | bytes 1572872 | tf_op jit(solution)/shard_map/ppermute | solution.py:34
  17.7 2.7 %convert_bitcast_fusion.2 = bf16[1024,1024]{0,1:T(8,128)(2,1)S(1)} fusion(f32[1024,1024]{1,0:T(8,128)} %param.10), kind=kLoop, calls=%fused_computation.74 | loop fusion | flops 1048576 | bytes 6291456 | tf_op jit(solution)/shard_map/transpose | solution.py:182
  20.4 4.4 %collective-permute-done.1 = f32[128,2,512]{2,1,0:T(2,128)S(1)} collective-permute-done((f32[128,2,512]{2,1,0:T(2,128)}, f32[128,2,512]{2,1,0:T(2,128)S(1)}, u32[]{:S(2)}, u32[]{:S(2)}) %collective-permute-start.1) | collective-permute-done | bytes 524320 | tf_op jit(solution)/shard_map/ppermute | solution.py:34
  24.7 12.1 %collective-permute-done = f32[128,2,512]{2,1,0:T(2,128)S(1)} collective-permute-done((f32[128,2,512]{2,1,0:T(2,128)}, f32[128,2,512]{2,1,0:T(2,128)S(1)}, u32[]{:S(2)}, u32[]{:S(2)}) %collective-permute-start) | collective-permute-done | bytes 524320 | tf_op jit(solution)/shard_map/ppermute | solution.py:33
  36.8 2.6 %pad_maximum_fusion.9 = (f32[128,20,2]{2,1,0:T(8,128)}, f32[128,20,2]{2,1,0:T(8,128)}) fusion(f32[128,2,512]{2,1,0:T(2,128)S(1)} %collective-permute-done.1, f32[128,16,512]{2,1,0:T(8,128)S(1)} %copy-done, f32[128,2,512]{2,1,0:T(2,128)S(1)} %collective-permute-done), kind=kLoop, calls=%fused_computation.31 | loop fusion | flops 20480 | bytes 5283840 | tf_op jit(solution)/shard_map/slice | solution.py:31
  39.5 1.8 copy.33
  47.3 3.9 %convert_element_type.72.w2 = bf16[1024,1024]{1,0:T(8,128)(2,1)} convert(f32[1024,1024]{1,0:T(8,128)} %param.10) | non-fusion elementwise | flops 1048576 | bytes 6291456 | tf_op jit(solution)/shard_map/convert_element_type | solution.py:160
  51.9 1.9 copy.38
  53.7 2.6 %copy.39.w2t = bf16[1024,1024]{1,0:T(8,128)(2,1)} copy(bf16[1024,1024]{0,1:T(8,128)(2,1)S(1)} %convert_bitcast_fusion.2) | data formatting | bytes 4194304 | tf_op jit(solution)/shard_map/transpose | solution.py:182
  57.7 2.4 %copy.34 = f32[128,20,2]{2,1,0:T(8,128)} copy(f32[128,20,2]{0,2,1:T(2,128)} %collective-permute-done.2) | data formatting | bytes 40960 | tf_op jit(solution)/shard_map/ppermute | solution.py:33
  60.1 7.9 %pad_maximum_fusion.6 = f32[128,20,516]{2,1,0:T(8,128)S(1)} fusion(f32[128,20,2]{2,1,0:T(8,128)S(1)} %copy.35, f32[128,2,512]{2,1,0:T(2,128)S(1)} %collective-permute-done.1, f32[128,16,512]{2,1,0:T(8,128)} %state.1, f32[128,2,512]{2,1,0:T(2,128)S(1)} %collective-permute-done, f32[128,20,2]{2,1,0:T(8,128)} %copy.34), kind=kLoop, calls=%fused_computation.12 | loop fusion | flops 5283840 | bytes 10567680 | tf_op jit(solution)/shard_map/concatenate | solution.py:35
  68.0 13.7 %fusion.3 = f32[128,18,514]{2,1,0:T(8,128)S(1)} fusion(f32[128,20,2]{2,1,0:T(8,128)S(1)} %copy.35, f32[128,2,512]{2,1,0:T(2,128)S(1)} %collective-permute-done.1, f32[128,16,512]{2,1,0:T(8,128)S(1)} %copy-done.1, f32[128,2,512]{2,1,0:T(2,128)S(1)} %collective-permute-done, f32[128,20,2]{2,1,0:T(8,128)} %copy.34, f32[128,20,516]{2,1,0:T(8,128)S(1)} %pad_maximum_fusion.6, ...), kind=kLoop, calls=%fused_computation.4 | loop fusion | flops 15395328 | bytes 24232448 | tf_op jit(solution)/shard_map/add | solution.py:43
  81.7 6.0 %fusion.7.after = f32[128,16,512]{2,1,0:T(8,128)} fusion(f32[128,18,514]{2,1,0:T(8,128)S(1)} %fusion.3, f32[128]{0:T(128)S(1)} %copy-done.8), kind=kLoop, calls=%fused_computation.17 | loop fusion | flops 7340032 | bytes 25166336 | tf_op jit(solution)/shard_map/add | solution.py:43
  87.7 22.4 %network.1 = (f32[8,128,128]{2,1,0:T(8,128)}, f32[8,1024,128]{2,1,0:T(8,128)}, f32[1024,128]{1,0:T(8,128)}) custom-call(s32[33]{0:T(128)} %pad_add_fusion.meta, f32[128,16,512]{2,1,0:T(8,128)} %state.1, f32[128,16,512]{2,1,0:T(8,128)} %fusion.7.after, bf16[1024,128]{1,0:T(8,128)(2,1)} %bitcast.63, bf16[1024,1024]{1,0:T(8,128)(2,1)} %copy.39.w2t, ...), custom_call_target="tpu_custom_call" | custom-call | tf_op jit(solution)/shard_map/network/pallas_call | solution.py:164
  114.0 3.2 %collective-permute-done.4 = bf16[5632,128]{1,0:T(8,128)(2,1)S(1)} collective-permute-done((bf16[5632,128]{1,0:T(8,128)(2,1)S(1)}, bf16[5632,128]{1,0:T(8,128)(2,1)S(1)}, u32[]{:S(2)}, u32[]{:S(2)}) %collective-permute-start.4) | collective-permute-done | bytes 1441824 | tf_op jit(solution)/shard_map/ppermute | solution.py:199
  119.0 22.5 %all_to_all.36 = bf16[4,1408,128]{2,1,0:T(8,128)(2,1)S(1)} all-to-all(bf16[4,1408,128]{2,1,0:T(8,128)(2,1)S(1)} %bitcast.56), channel_id=1, replica_groups=mesh['z'=4,'y'=4,'xh'=2,'xl'=2,'c'=2] {'xh','xl'}, dimensions={0} | all-to-all | bytes 2883584 | tf_op jit(solution)/shard_map/all_to_all | solution.py:206
  141.7 38.8 %all_to_all.37 = f32[16,88,128]{2,1,0:T(8,128)S(1)} all-to-all(f32[16,88,128]{2,1,0:T(8,128)S(1)} %bitcast.57), channel_id=1, replica_groups=mesh['z'=4,'y'=4,'xh'=2,'xl'=2,'c'=2] {'z','y'}, dimensions={0} | all-to-all | bytes 1441792 | tf_op jit(solution)/shard_map/all_to_all | solution.py:208
  182.0 11.0 %all_to_all.38 = f16[16,96,128]{2,1,0:T(8,128)(2,1)S(1)} all-to-all(f16[16,96,128]{2,1,0:T(8,128)(2,1)S(1)} %broadcast_in_dim.53), channel_id=1, replica_groups=mesh['z'=4,'y'=4,'xh'=2,'xl'=2,'c'=2] {'z','y'}, dimensions={0} | all-to-all | bytes 786432 | tf_op jit(solution)/shard_map/all_to_all | solution.py:217
  193.3 19.3 %all_to_all.39 = f16[4,1536,128]{2,1,0:T(8,128)(2,1)S(1)} all-to-all(f16[4,1536,128]{2,1,0:T(8,128)(2,1)S(1)} %broadcast_in_dim.54), channel_id=1, replica_groups=mesh['z'=4,'y'=4,'xh'=2,'xl'=2,'c'=2] {'xh','xl'}, dimensions={0} | all-to-all | bytes 3145728 | tf_op jit(solution)/shard_map/all_to_all | solution.py:217
  212.6 4.9 %collective-permute-start.5 = (f16[6144,128]{1,0:T(8,128)(2,1)S(1)}, f16[6144,128]{1,0:T(8,128)(2,1)S(1)}, u32[]{:S(2)}, u32[]{:S(2)}) collective-permute-start(f16[6144,128]{1,0:T(8,128)(2,1)S(1)} %bitcast.54), channel_id=1, source_target_pairs={{0,1},{1,0},{2,3},{3,2},{4,5},{5,4},{6,7},{7,6},{8,9},{9,8},{10,11... | collective-permute-start | bytes 4718600 | tf_op jit(solution)/shard_map/ppermute | solution.py:218
  217.9 2.6 %collective-permute-done.5 = f16[6144,128]{1,0:T(8,128)(2,1)S(1)} collective-permute-done((f16[6144,128]{1,0:T(8,128)(2,1)S(1)}, f16[6144,128]{1,0:T(8,128)(2,1)S(1)}, u32[]{:S(2)}, u32[]{:S(2)}) %collective-permute-start.5) | collective-permute-done | bytes 1572896 | tf_op jit(solution)/shard_map/ppermute | solution.py:218
  225.0 1.9 copy-done.2
  226.9 2.6 %bitcast_subtract_fusion = f32[1024,1024]{1,0:T(8,128)} fusion(f32[1024,1024]{1,0:T(8,128)S(1)} %copy-done.2, f32[8,128,8,128]{3,2,1,0:T(8,128)S(1)} %bitcast.49), kind=kLoop, calls=%fused_computation.13 | loop fusion | flops 1048576 | bytes 12582912 | tf_op jit(solution)/shard_map/sub | solution.py:259
  (65 shorter events, 23.6 us)
Async XLA Ops:
  4.3 20.4 %collective-permute-start.1 = (f32[128,2,512]{2,1,0:T(2,128)}, f32[128,2,512]{2,1,0:T(2,128)S(1)}, u32[]{:S(2)}, u32[]{:S(2)}) collective-permute-start(f32[128,2,512]{2,1,0:T(2,128)} %get-tuple-element.17), channel_id=1, source_target_pairs={{4,0},{8,4},{12,8},{16,12},{20,16},{24,20},{28,24},{32,28},{36,32}... | collective-permute-start | bytes 1572872 | tf_op jit(solution)/shard_map/ppermute | solution.py:34
  13.8 23.0 %collective-permute-start = (f32[128,2,512]{2,1,0:T(2,128)}, f32[128,2,512]{2,1,0:T(2,128)S(1)}, u32[]{:S(2)}, u32[]{:S(2)}) collective-permute-start(f32[128,2,512]{2,1,0:T(2,128)} %get-tuple-element.16), channel_id=1, source_target_pairs={{0,4},{4,8},{8,12},{12,16},{16,20},{20,24},{24,28},{28,32},{32,36}... | collective-permute-start | bytes 1572872 | tf_op jit(solution)/shard_map/ppermute | solution.py:33
  17.7 19.2 %copy-start = (f32[128,16,512]{2,1,0:T(8,128)S(1)}, f32[128,16,512]{2,1,0:T(8,128)}, u32[]{:S(2)}) copy-start(f32[128,16,512]{2,1,0:T(8,128)} %state.1) | copy-start | bytes 12582916
  41.3 15.9 %collective-permute-start.3 = (f32[128,20,2]{0,2,1:T(2,128)S(1)}, f32[128,20,2]{0,2,1:T(2,128)S(1)}, u32[]{:S(2)}, u32[]{:S(2)}) collective-permute-start(f32[128,20,2]{0,2,1:T(2,128)S(1)} %copy.33), channel_id=1, source_target_pairs={{1,0},{2,1},{3,2},{0,3},{5,4},{6,5},{7,6},{4,7},{9,8},{10,9},{11,1... | collective-permute-start | bytes 61448 | tf_op jit(solution)/shard_map/ppermute | solution.py:34
  44.7 13.0 %collective-permute-start.2 = (f32[128,20,2]{0,2,1:T(2,128)S(1)}, f32[128,20,2]{0,2,1:T(2,128)}, u32[]{:S(2)}, u32[]{:S(2)}) collective-permute-start(f32[128,20,2]{0,2,1:T(2,128)S(1)} %copy.32), channel_id=1, source_target_pairs={{0,1},{1,2},{2,3},{3,0},{4,5},{5,6},{6,7},{7,4},{8,9},{9,10},{10,1... | collective-permute-start | bytes 61448 | tf_op jit(solution)/shard_map/ppermute | solution.py:33
  47.3 3.9 %copy-start.3 = (f32[1024,128]{1,0:T(8,128)S(1)}, f32[1024,128]{1,0:T(8,128)}, u32[]{:S(2)}) copy-start(f32[1024,128]{1,0:T(8,128)} %param.11) | copy-start | bytes 1572868
  60.1 7.9 %copy-start.1 = (f32[128,16,512]{2,1,0:T(8,128)S(1)}, f32[128,16,512]{2,1,0:T(8,128)}, u32[]{:S(2)}) copy-start(f32[128,16,512]{2,1,0:T(8,128)} %state.1) | copy-start | bytes 12582916
  60.1 7.9 %copy-start.8 = (f32[128]{0:T(128)S(1)}, f32[128]{0:T(128)}, u32[]{:S(2)}) copy-start(f32[128]{0:T(128)} %param.8) | copy-start | bytes 1540
  113.8 3.6 %copy-start.7 = (f32[1024,128]{1,0:T(8,128)S(1)}, f32[1024,128]{1,0:T(8,128)}, u32[]{:S(2)}) copy-start(f32[1024,128]{1,0:T(8,128)} %get-tuple-element.9) | copy-start | bytes 1572868
  113.9 3.3 %collective-permute-start.4 = (bf16[5632,128]{1,0:T(8,128)(2,1)S(1)}, bf16[5632,128]{1,0:T(8,128)(2,1)S(1)}, u32[]{:S(2)}, u32[]{:S(2)}) collective-permute-start(bf16[5632,128]{1,0:T(8,128)(2,1)S(1)} %pad_maximum_fusion.10), channel_id=1, source_target_pairs={{0,1},{1,0},{2,3},{3,2},{4,5},{5,4},{6,7},{7,6},{8,9},{9,8},{10,11... | collective-permute-start | bytes 4325384 | tf_op jit(solution)/shard_map/ppermute | solution.py:199
  114.0 4.5 %copy-start.5 = (f32[8,1024,128]{2,1,0:T(8,128)S(1)}, f32[8,1024,128]{2,1,0:T(8,128)}, u32[]{:S(2)}) copy-start(f32[8,1024,128]{2,1,0:T(8,128)} %get-tuple-element.8) | copy-start | bytes 12582916
  212.6 7.9 %collective-permute-start.5 = (f16[6144,128]{1,0:T(8,128)(2,1)S(1)}, f16[6144,128]{1,0:T(8,128)(2,1)S(1)}, u32[]{:S(2)}, u32[]{:S(2)}) collective-permute-start(f16[6144,128]{1,0:T(8,128)(2,1)S(1)} %bitcast.54), channel_id=1, source_target_pairs={{0,1},{1,0},{2,3},{3,2},{4,5},{5,4},{6,7},{7,6},{8,9},{9,8},{10,11... | collective-permute-start | bytes 4718600 | tf_op jit(solution)/shard_map/ppermute | solution.py:218
  221.9 1.0 copy-start.4
  222.0 1.9 copy-start.6
  224.7 2.2 copy-start.2

commit v2 on v1

v2 whole, which is shorter than its diff:
```python
import functools
import math

import jax
import jax.numpy as jnp
from jax import lax
from jax.experimental import pallas as pl
from jax.experimental.pallas import tpu as pltpu
from jax.sharding import Mesh
from jax.sharding import PartitionSpec as P

BW = 128
RATE = 0.5
TARGET_GAIN = 4.0
STEP = 4
SHARDS = 64

SIM = ("z", "y", "xh")
LEARN = ("xl", "c")
RING = ("xh", "xl")
PLANE = ("z", "y")

BF16 = jnp.bfloat16
F32 = jnp.float32


def shift(x, axis, by):
    size = lax.axis_size(axis)
    return lax.ppermute(x, axis, [(i, (i + by) % size) for i in range(size)])


def stencil_kernel(diffusion, state, edge_rows, edge_cols, corners, after, even, odd):
    chunk, rows, cols = state.shape
    base = pl.program_id(0) * chunk
    tall, wide = rows + 8, cols + BW

    def diffuse(field, at):
        rate = diffusion[base + at]
        beside = pltpu.roll(field, 1, 0) + pltpu.roll(field, tall - 1, 0)
        beside = beside + pltpu.roll(field, 1, 1) + pltpu.roll(field, wide - 1, 1)
        return (1.0 - 4.0 * rate) * field + rate * beside

    def first(at, held):
        upper = jnp.concatenate([state[at], edge_cols[at]], axis=1)
        lower = jnp.concatenate([edge_rows[at], corners[at]], axis=1)
        held[...] = diffuse(jnp.concatenate([upper, lower], axis=0), at)

    def second(at, held):
        after[at] = diffuse(held[...], at)[:rows, :cols]

    first(0, even)

    def pair(at, carry):
        first(2 * at + 1, odd)
        second(2 * at, even)
        first(jnp.minimum(2 * at + 2, chunk - 1), even)
        second(2 * at + 1, odd)
        return carry

    lax.fori_loop(0, chunk // 2, pair, 0, unroll=2)


def diffuse_twice(state, diffusion, later):
    levels, rows, cols = state.shape
    half = jnp.float16
    left = shift(jnp.transpose(state[:, :, cols - 2 :], (2, 1, 0)), LEARN, 1)
    right = shift(jnp.transpose(state[:, :, :2], (2, 1, 0)), LEARN, -1)

    def outgoing(first, at):
        ends = jnp.concatenate([left[1, at], right[0, at], jnp.zeros((cols - 2 * levels,), F32)])
        ends = jnp.stack([ends, jnp.zeros_like(ends)])[None]
        return jnp.concatenate([state[:, first : first + 2], ends]).astype(half)

    ends = (outgoing(rows - 2, rows - 1), outgoing(0, 0))
    ends, later = lax.optimization_barrier((ends, later))
    above = shift(ends[0], SIM, 1)
    below = shift(ends[1], SIM, -1)
    edge_cols = jnp.concatenate([right, jnp.zeros((BW - 4, rows, levels), F32), left])
    edge_cols = jnp.transpose(edge_cols, (2, 1, 0))
    gap = jnp.zeros((levels, 4, cols), F32)
    edge_rows = jnp.concatenate(
        [below[:levels].astype(F32), gap, above[:levels].astype(F32)], axis=1
    )
    row = lax.broadcasted_iota(jnp.int32, (levels, 8, BW), 1)
    lane = lax.broadcasted_iota(jnp.int32, (levels, 8, BW), 2)
    corners = jnp.zeros((levels, 8, BW), F32)
    for at, block in ((0, below), (7, above)):
        ends = block[levels, 0].astype(F32)
        for spot, value in ((BW - 1, ends[:levels]), (0, ends[levels : 2 * levels])):
            corners = jnp.where((row == at) & (lane == spot), value[:, None, None], corners)
    return stencil_call(state, edge_rows, edge_cols, corners, diffusion), later


def stencil_call(state, edge_rows, edge_cols, corners, diffusion):
    levels, rows, cols = state.shape
    chunk = 16

    def block(*shape):
        return pl.BlockSpec((chunk,) + shape, lambda i: (i, 0, 0))

    return pl.pallas_call(
        stencil_kernel,
        out_shape=jax.ShapeDtypeStruct(state.shape, F32),
        grid=(levels // chunk,),
        in_specs=[
            pl.BlockSpec(memory_space=pltpu.SMEM),
            block(rows, cols),
            block(8, cols),
            block(rows, BW),
            block(8, BW),
        ],
        out_specs=block(rows, cols),
        scratch_shapes=[pltpu.VMEM((rows + 8, cols + BW), F32)] * 2,
        name="stencil",
    )(diffusion, state, edge_rows, edge_cols, corners)


def dot(a, b):
    return jnp.dot(a, b, preferred_element_type=F32)


def dot_t(a, b):
    return lax.dot_general(a, b, (((1,), (1,)), ((), ())), preferred_element_type=F32)


def activate(value):
    sigma = 0.5 * jnp.tanh(0.5 * value) + 0.5
    act = value * sigma
    return act.astype(BF16), sigma + act * (1.0 - sigma)


def store_split(target, block):
    high = block.astype(BF16)
    low = (block[:, 72:] - high[:, 72:].astype(F32)).astype(BF16)
    target[:, :80], target[:, 80:] = high, low


def network_kernel(
    count, meta, state, after, w1t, w2t, w2, w3t, w3, grads, send, xbuf, abuf, slope1, slope2, sems
):
    total, core = meta[0], meta[1]
    steps = (total + STEP - 1) // STEP
    per_row = state.shape[2] // BW
    levels = w1t.shape[1]
    hid = w2.shape[0]

    def copies(step, slot, i):
        spot = meta[2 + step * STEP + i]
        row, col = spot // per_row, pl.multiple_of((spot % per_row) * BW, BW)
        lanes = pl.ds(i * BW, BW)
        return (
            pltpu.make_async_copy(
                state.at[:, row, pl.ds(col, BW)], xbuf.at[slot, :, lanes], sems.at[slot, i, 0]
            ),
            pltpu.make_async_copy(
                after.at[:, row, pl.ds(col, BW)], abuf.at[slot, :, lanes], sems.at[slot, i, 1]
            ),
        )

    def fetch(step, slot):
        for i in range(STEP):

            @pl.when(step * STEP + i < total)
            def _():
                for copy in copies(step, slot, i):
                    copy.start()

    @pl.when(steps > 0)
    def _():
        fetch(0, 0)

    grads[...] = jnp.zeros_like(grads)

    def body(step, carry):
        slot = lax.rem(step, 2)

        @pl.when(step + 1 < steps)
        def _():
            fetch(step + 1, 1 - slot)

        for i in range(STEP):
            index = step * STEP + i

            @pl.when(index < total)
            def _():
                for copy in copies(step, slot, i):
                    copy.wait()

            @pl.when(index >= total)
            def _():
                zero = jnp.zeros((levels, BW), F32)
                xbuf[slot, :, i * BW : (i + 1) * BW] = zero
                abuf[slot, :, i * BW : (i + 1) * BW] = zero

        x = xbuf[slot]
        inputs = x.astype(BF16)
        targets = (TARGET_GAIN * (abuf[slot] - x)).astype(BF16)
        act_one, slope1[...] = activate(dot(w1t[...], inputs))
        act_two, slope2[...] = activate(dot(w2t[...], act_one))
        output = dot(w3t[...], act_two)
        error = ((output - targets.astype(F32)) / count).astype(BF16)
        grads[:, :, :, 72:] += dot_t(act_two, error).reshape(2, 8, 8, 8, BW)
        delta_two = (dot(w3[...], error) * slope2[...]).astype(BF16)
        for j in range(0, hid // BW, 2):
            both = dot_t(act_one, delta_two[j * BW : (j + 2) * BW])
            for k in (0, 1):
                at = (j + k) * 8
                grads[:, :, :, at : at + 8] += both[:, k * BW : (k + 1) * BW].reshape(2, 8, 8, 8, BW)
        delta_one = (dot(w2[...], delta_two) * slope1[...]).astype(BF16)
        for j in range(0, hid // BW, 2):
            both = dot_t(inputs, delta_one[j * BW : (j + 2) * BW])
            for k in (0, 1):
                grads[:, :, j + k, 64:72] += both[:, k * BW : (k + 1) * BW].reshape(2, 8, 8, BW)
        return carry

    lax.fori_loop(0, steps, body, 0)
    store_split(send, grads[1 - core].reshape(SHARDS, 80, BW))


def network(meta, state, after, weight_in, weight_mid, weight_out, count):
    levels, hid = weight_in.shape
    first, second, third = (w.astype(BF16) for w in (weight_in, weight_mid, weight_out))
    vmem = pl.BlockSpec(memory_space=pltpu.VMEM)
    hbm = pl.BlockSpec(memory_space=pl.ANY)
    width = STEP * BW
    return pl.pallas_call(
        functools.partial(network_kernel, count),
        out_shape=(
            jax.ShapeDtypeStruct((2, 8, 8, 80, BW), F32),
            jax.ShapeDtypeStruct((SHARDS, 88, BW), BF16),
        ),
        in_specs=[pl.BlockSpec(memory_space=pltpu.SMEM), hbm, hbm] + [vmem] * 5,
        out_specs=(vmem, vmem),
        scratch_shapes=[
            pltpu.VMEM((2, levels, width), F32),
            pltpu.VMEM((2, levels, width), F32),
            pltpu.VMEM((hid, width), F32),
            pltpu.VMEM((hid, width), F32),
            pltpu.SemaphoreType.DMA((2, STEP, 2)),
        ],
        compiler_params=pltpu.CompilerParams(vmem_limit_bytes=56 * 1024 * 1024),
        name="network",
    )(meta, state, after, first.T, second.T, second, third.T, third)


def update_kernel(half, total, w_in, w_mid, w_out, *rest):
    new_in, new_mid, new_out = rest[-3:]
    for a in range(total.shape[0]):
        for b in range(8):
            step = RATE * total[a, b]
            lanes = slice(b * BW, (b + 1) * BW)
            rows = slice(a * 8, (a + 1) * 8)
            new_in[rows, lanes] = w_in[rows, lanes] - step[64:72]
            rows = slice(a * 64 + b * 8, a * 64 + (b + 1) * 8)
            new_out[rows, :] = w_out[rows, :] - step[72:]
            for j in range(8):
                lanes = slice(j * BW, (j + 1) * BW)
                new_mid[rows, lanes] = w_mid[rows, lanes] - step[j * 8 : (j + 1) * 8]


def update(half, total, weights, news):
    hid = weights[1].shape[0]
    a = 2
    steps = 8 // a
    blocks = [
        pl.BlockSpec((8 * a, hid), lambda i, half: (half[0] * steps + i, 0)),
        pl.BlockSpec((64 * a, hid), lambda i, half: (half[0] * steps + i, 0)),
        pl.BlockSpec((64 * a, BW), lambda i, half: (half[0] * steps + i, 0)),
    ]
    kept = [pl.BlockSpec(memory_space=pl.ANY)] * len(news)
    return pl.pallas_call(
        update_kernel,
        out_shape=[jax.ShapeDtypeStruct(w.shape, F32) for w in weights],
        grid_spec=pltpu.PrefetchScalarGridSpec(
            num_scalar_prefetch=1,
            grid=(steps,),
            in_specs=[pl.BlockSpec((a, 8, 80, BW), lambda i, half: (i, 0, 0, 0))] + blocks + kept,
            out_specs=blocks,
        ),
        input_output_aliases={5 + i: i for i in range(len(news))},
        cost_estimate=pl.CostEstimate(flops=20_000_000, bytes_accessed=8_000_000, transcendentals=0),
        name="update",
    )(half[None], total, *weights, *news)


def sum_everywhere(grads, send, weights):
    core = lax.axis_index("c")
    swap = [(0, 1), (1, 0)]
    got = lax.ppermute(send, "c", swap).astype(F32)
    pair = lax.dynamic_index_in_dim(grads, core, 0, False).reshape(SHARDS, 80, BW)
    pair = pair + got[:, :80]
    last = pair[:, 72:] + got[:, 80:]
    high = lax.reduce_precision(last, 8, 7)
    pair = jnp.concatenate([pair[:, :72], high, last - high], axis=1).astype(BF16)
    ring, plane = lax.axis_size(RING), lax.axis_size(PLANE)
    held = lax.all_to_all(pair.reshape(-1, BW), PLANE, 0, 0, tiled=True)
    held = jnp.sum(held.reshape(plane, -1, BW).astype(F32), axis=0)
    held = lax.all_to_all(held, RING, 0, 0, tiled=True)
    held = jnp.sum(held.reshape(ring, -1, BW), axis=0)
    held = jnp.concatenate([held[:72], held[72:80] + held[80:]])
    power = jnp.floor(jnp.log2(jnp.maximum(jnp.max(jnp.abs(held)), 1e-30)))
    sent = (held * jnp.exp2(14.0 - power)).astype(jnp.float16)
    sent = jnp.concatenate([sent, jnp.full((8, BW), power, jnp.float16)])
    for axis, size in ((RING, ring), (PLANE, plane)):
        spread = jnp.broadcast_to(sent, (size,) + sent.shape).reshape(-1, BW)
        sent = lax.all_to_all(spread, axis, 0, 0, tiled=True)
    away = lax.ppermute(sent, "c", swap)

    def opened(block):
        block = block.reshape(SHARDS, 88, BW).astype(F32)
        return (block[:, :80] * jnp.exp2(block[:, 80:81] - 14.0)).reshape(8, 8, 80, BW)

    news = update(core, opened(sent), weights, ())
    return update(1 - core, opened(away), weights, news)


def on_device(state_field, diffusion, weight_in, weight_mid, weight_out, block_tile, block_pos):
    levels, tile_rows, tile_cols = state_field.shape
    weights = (weight_in, weight_mid, weight_out)
    after, late = diffuse_twice(state_field, diffusion, (weights, block_tile, block_pos))
    late_weights, block_tile, block_pos = late
    senders = lax.axis_size(SIM)
    own_index = lax.axis_index(SIM)
    samples = block_tile.shape[0] // senders
    tiles = block_tile[:, 0].reshape(senders, samples)
    places = block_pos.reshape(senders, samples)
    matched = tiles == own_index
    place = jnp.sum(jnp.where(matched, places, 0), axis=1)
    present = jnp.any(matched, axis=1)
    order = jnp.arange(senders)
    rank = jnp.sum(jnp.where(order[None, :] < order[:, None], present[None, :], False), axis=1)
    lands = present[:, None] & (rank[:, None] == order[None, :])
    slots = jnp.sum(jnp.where(lands, place[:, None], 0), axis=0)
    total = jnp.sum(present.astype(jnp.int32))
    meta = jnp.concatenate([jnp.stack([total, lax.axis_index("c")]), slots.astype(jnp.int32)])
    count = float(senders * lax.axis_size(LEARN) * samples * BW)
    grads, send = network(meta, state_field, after, *late_weights, count)
    new_in, new_mid, new_out = sum_everywhere(grads, send, weights)
    return (after, new_in, new_mid, new_out)


def solution(mesh):
    fine = Mesh(mesh.devices.reshape(4, 4, 2, 2, 2), SIM + LEARN)
    placed = (P(None, SIM, LEARN), P(), P(), P(), P(), P(LEARN, None), P(LEARN))
    return jax.shard_map(
        on_device,
        mesh=fine,
        in_specs=placed,
        out_specs=(P(None, SIM, LEARN), P(), P(), P()),
        check_vma=False,
    )
```

time: 231 us -> 189 us (0.82)
  other arithmetic: 51.8 us -> 21.9 us
  Pallas kernels: 22.4 us -> 39.3 us
  blocking collectives: 91.6 us -> 77.6 us
  waiting for transfers between devices: 22.2 us -> 9.93 us
  local copies, waits for them, and re-layouts: 22.4 us -> 11.4 us
  starting transfers between devices: 17.3 us -> 27.4 us
    pallas_call x0 -> x3, Pallas kernels: none -> 22.1 us  [the longest x1 13.2 us: stencil_call(): pl.pallas_call(stencil_kernel, out_shape=jax.ShapeDtypeStruct(state.shape...]
    add x4 -> x2, other arithmetic: 19.8 us -> 0.26 us  [the longest x1 0.26 us: sum_everywhere(): pair = pair + got[:, :80]]
    ppermute x6, waiting for transfers between devices: 22.2 us -> 9.93 us  [the longest x4 8.8 us: shift(): return lax.ppermute(x, axis, [(i, (i + by) % size) for i in range(size)])]
    all_to_all x2, blocking collectives: 61.3 us -> 49.5 us  [the longest x1 42 us: sum_everywhere(): held = lax.all_to_all(pair.reshape(-1, BW), PLANE, 0, 0, tiled=True)]
    ppermute x6, starting transfers between devices: 17.3 us -> 27.4 us  [the longest x1 11.7 us: sum_everywhere(): got = lax.ppermute(send, 'c', swap).astype(F32)]
    pallas_call x1, Pallas kernels: 22.4 us -> 17.1 us  [network(): pl.pallas_call(functools.partial(network_kernel, count), out_shape=(jax.S...]
    slice x5 -> x6, local copies, waits for them, and re-layouts: 7.6 us -> 2.62 us  [the longest x1 1.9 us: diffuse_twice(): left = shift(jnp.transpose(state[:, :, cols - 2:], (2, 1, 0)), LEARN, 1)]
    concatenate x4 -> x5, other arithmetic: 9.37 us -> 4.59 us  [the longest x1 1.81 us: diffuse_twice(): jnp.concatenate([below[:levels].astype(F32), gap, above[:levels].astype(F...]
  transfers between devices with their start and end apart: 6 -> 6, of which waited for: 4 -> 2; matrix products, arithmetic and copies ran while one was open for 9% -> 11% of each run, Pallas kernels for 0% -> 2%
where the time goes in v2:
time: 189 us
  blocking collectives  77.6 us (41%)
  Pallas kernels  39.3 us (21%)
  starting transfers between devices  27.4 us (14%)
  other arithmetic  21.9 us (12%)
  local copies, waits for them, and re-layouts  11.4 us (6%)
  waiting for transfers between devices  9.93 us (5%)
    all_to_all x1, blocking collectives, sum_everywhere(): held = lax.all_to_all(pair.reshape(-1, BW), PLANE, 0, 0, tiled=True)  42 us
    all_to_all x2, blocking collectives, sum_everywhere(): sent = lax.all_to_all(spread, axis, 0, 0, tiled=True)  28.1 us
    pallas_call x1, Pallas kernels, network(): pl.pallas_call(functools.partial(network_kernel, count), out_shape=(jax.S...  17.1 us
    pallas_call x1, Pallas kernels, stencil_call(): pl.pallas_call(stencil_kernel, out_shape=jax.ShapeDtypeStruct(state.shape...  13.2 us
    ppermute x1, starting transfers between devices, sum_everywhere(): got = lax.ppermute(send, 'c', swap).astype(F32)  11.7 us
    ppermute x4, starting transfers between devices, shift(): return lax.ppermute(x, axis, [(i, (i + by) % size) for i in range(size)])  11.4 us
    pallas_call x2, Pallas kernels, update(): pl.pallas_call(update_kernel, out_shape=[jax.ShapeDtypeStruct(w.shape, F3...  8.89 us
    ppermute x4, waiting for transfers between devices, shift(): return lax.ppermute(x, axis, [(i, (i + by) % size) for i in range(size)])  8.8 us
  transfers between devices with their start and end apart: 6, of which 2 were waited for; matrix products, arithmetic and copies ran while one was open for 11% of the time, Pallas kernels for 2%

profile of v2, /device:TPU:1, one launch (start us, length us, event | category | flops | bytes accessed | tf_op | source)
XLA Modules:
  0.0 189.2 jit_solution(13058738719230808655)
XLA Ops:
  0.6 1.9 %fusion.7 = (f32[128,16,2]{2,1,0:T(8,128)S(1)}, f32[128,16,2]{2,1,0:T(8,128)S(1)}) fusion(f32[128,16,512]{2,1,0:T(8,128)} %state.3), kind=kLoop, calls=%fused_computation.57 | loop fusion | bytes 65536 | tf_op jit(solution)/shard_map/slice | solution.py:66
  3.0 1.4 collective-permute-start.1
  6.1 2.8 %convert.48 = f16[128,16,512]{2,1,0:T(8,128)(2,1)S(1)} convert(f32[128,16,512]{2,1,0:T(8,128)} %state.3) | non-fusion elementwise | flops 1048576 | bytes 6291456 | tf_op jit(solution)/shard_map/convert.33
  9.8 1.4 pad_maximum_fusion.2
  12.5 8.7 %collective-permute-start.2 = (f16[129,2,512]{2,1,0:T(2,128)(2,1)}, f16[129,2,512]{2,1,0:T(2,128)(2,1)S(1)}, u32[]{:S(2)}, u32[]{:S(2)}) collective-permute-start(f16[129,2,512]{2,1,0:T(2,128)(2,1)} %get-tuple-element.19), channel_id=1, source_target_pairs={{0,124},{4,0},{8,4},{12,8},{16,12},{20,16},{24,20},{28,24},{32,28}... | collective-permute-start | bytes 792584 | tf_op jit(solution)/shard_map/ppermute | solution.py:29
  21.2 2.5 %convert_bitcast_fusion.2 = bf16[1024,1024]{0,1:T(8,128)(2,1)S(1)} fusion(f32[1024,1024]{1,0:T(8,128)} %w_mid.3), kind=kLoop, calls=%fused_computation.60 | loop fusion | flops 1048576 | bytes 6291456 | tf_op jit(solution)/shard_map/transpose | solution.py:243
  25.8 1.7 convert_element_type.68.w2
  29.2 2.6 %copy.32.w2t = bf16[1024,1024]{1,0:T(8,128)(2,1)} copy(bf16[1024,1024]{0,1:T(8,128)(2,1)S(1)} %convert_bitcast_fusion.2) | data formatting | bytes 4194304 | tf_op jit(solution)/shard_map/transpose | solution.py:243
  34.1 8.8 %collective-permute-done.3 = f16[129,2,512]{2,1,0:T(2,128)(2,1)S(1)} collective-permute-done((f16[129,2,512]{2,1,0:T(2,128)(2,1)S(1)}, f16[129,2,512]{2,1,0:T(2,128)(2,1)S(1)}, u32[]{:S(2)}, u32[]{:S(2)}) %collective-permute-start.3) | collective-permute-done | bytes 264224 | tf_op jit(solution)/shard_map/ppermute | solution.py:29
  43.3 1.8 pad_maximum_fusion.edge_rows
  45.1 1.4 select_select_fusion.corners
  46.5 13.2 %stencil.1.after = f32[128,16,512]{2,1,0:T(8,128)} custom-call(f32[128]{0:T(128)} %diffusion.1, f32[128,16,512]{2,1,0:T(8,128)} %state.3, f32[128,8,512]{2,1,0:T(8,128)} %pad_maximum_fusion.edge_rows, f32[128,16,128]{2,1,0:T(8,128)} %maximum_bitcast_fusion.edge_cols, f32[128,8,128]{2,1,0:T(8,128)} %select_select_fusion.corners), custom_call_target="tpu_custom_call" | custom-call | tf_op jit(solution)/shard_map/stencil/pallas_call | solution.py:101
  59.8 17.1 %network.1 = (f32[2,8,8,80,128]{4,3,2,1,0:T(8,128)}, bf16[64,88,128]{2,1,0:T(8,128)(2,1)}) custom-call(s32[34]{0:T(128)} %pad_add_fusion.meta, f32[128,16,512]{2,1,0:T(8,128)} %state.3, f32[128,16,512]{2,1,0:T(8,128)} %stencil.1.after, bf16[1024,128]{1,0:T(8,128)(2,1)} %bitcast.54, bf16[1024,1024]{1,0:T(8,128)(2,1)} %copy.32.w2t, ...), custom_call_target="tpu_custom_call" | custom-call | tf_op jit(solution)/shard_map/network/pallas_call | solution.py:226
  76.9 11.7 %collective-permute-start.4 = (bf16[64,88,128]{2,1,0:T(8,128)(2,1)}, bf16[64,88,128]{2,1,0:T(8,128)(2,1)S(1)}, u32[]{:S(2)}, u32[]{:S(2)}) collective-permute-start(bf16[64,88,128]{2,1,0:T(8,128)(2,1)} %get-tuple-element.27), channel_id=1, source_target_pairs={{0,1},{1,0},{2,3},{3,2},{4,5},{5,4},{6,7},{7,6},{8,9},{9,8},{10,11... | collective-permute-start | bytes 4325384 | tf_op jit(solution)/shard_map/ppermute | solution.py:289
  88.6 1.9 %constant_dynamic-slice_fusion = f32[1,8,8,80,128]{4,3,2,1,0:T(8,128)S(1)} fusion(f32[2,8,8,80,128]{4,3,2,1,0:T(8,128)} %get-tuple-element.26, s32[]{:T(128)S(6)} %select_n.36), kind=kLoop, calls=%fused_computation.56 | loop fusion | bytes 5242884 | tf_op jit(solution)/shard_map/jit(dynamic_index_in_dim)/dynamic_slice | solution.py:290
  92.5 42.0 %all_to_all.33 = bf16[16,352,128]{2,1,0:T(8,128)(2,1)S(1)} all-to-all(bf16[16,352,128]{2,1,0:T(8,128)(2,1)S(1)} %bitcast.52), channel_id=1, replica_groups=mesh['z'=4,'y'=4,'xh'=2,'xl'=2,'c'=2] {'z','y'}, dimensions={0} | all-to-all | bytes 2883584 | tf_op jit(solution)/shard_map/all_to_all | solution.py:296
  134.7 7.5 %all_to_all.34 = f32[4,88,128]{2,1,0:T(8,128)S(1)} all-to-all(f32[4,88,128]{2,1,0:T(8,128)S(1)} %bitcast.55), channel_id=1, replica_groups=mesh['z'=4,'y'=4,'xh'=2,'xl'=2,'c'=2] {'xh','xl'}, dimensions={0} | all-to-all | bytes 360448 | tf_op jit(solution)/shard_map/all_to_all | solution.py:298
  143.6 7.0 %all_to_all.35 = f16[4,88,128]{2,1,0:T(8,128)(2,1)S(1)} all-to-all(f16[4,88,128]{2,1,0:T(8,128)(2,1)S(1)} %broadcast_in_dim.105), channel_id=1, replica_groups=mesh['z'=4,'y'=4,'xh'=2,'xl'=2,'c'=2] {'xh','xl'}, dimensions={0} | all-to-all | bytes 180224 | tf_op jit(solution)/shard_map/all_to_all | solution.py:306
  150.8 21.1 %all_to_all.36 = f16[16,352,128]{2,1,0:T(8,128)(2,1)S(1)} all-to-all(f16[16,352,128]{2,1,0:T(8,128)(2,1)S(1)} %broadcast_in_dim.106), channel_id=1, replica_groups=mesh['z'=4,'y'=4,'xh'=2,'xl'=2,'c'=2] {'z','y'}, dimensions={0} | all-to-all | bytes 2883584 | tf_op jit(solution)/shard_map/all_to_all | solution.py:306
  171.9 4.4 %collective-permute-start.5 = (f16[5632,128]{1,0:T(8,128)(2,1)S(1)}, f16[5632,128]{1,0:T(8,128)(2,1)S(1)}, u32[]{:S(2)}, u32[]{:S(2)}) collective-permute-start(f16[5632,128]{1,0:T(8,128)(2,1)S(1)} %bitcast.50), channel_id=1, source_target_pairs={{0,1},{1,0},{2,3},{3,2},{4,5},{5,4},{6,7},{7,6},{8,9},{9,8},{10,11... | collective-permute-start | bytes 4325384 | tf_op jit(solution)/shard_map/ppermute | solution.py:307
  176.6 1.7 slice_multiply_fusion
  178.3 4.4 %update.2 = (f32[128,1024]{1,0:T(8,128)}, f32[1024,1024]{1,0:T(8,128)}, f32[1024,128]{1,0:T(8,128)}) custom-call(s32[1]{0:T(128)} %bitcast.15.half, f32[8,8,80,128]{3,2,1,0:T(8,128)} %bitcast.49, f32[128,1024]{1,0:T(8,128)} %w_in.3, f32[1024,1024]{1,0:T(8,128)} %w_mid.3, f32[1024,128]{1,0:T(8,128)} %w_out.3), custom_call_target="tpu_custom_call" | custom-call | flops 20000000 | bytes 8000000 | tf_op jit(solution)/shard_map/update/pallas_call | solution.py:271
  183.0 1.7 slice_multiply_fusion.1
  184.7 4.4 %update.3 = (f32[128,1024]{1,0:T(8,128)}, f32[1024,1024]{1,0:T(8,128)}, f32[1024,128]{1,0:T(8,128)}) custom-call(s32[1]{0:T(128)} %bitcast.13.half, f32[8,8,80,128]{3,2,1,0:T(8,128)} %bitcast.48, f32[128,1024]{1,0:T(8,128)} %w_in.3, f32[1024,1024]{1,0:T(8,128)} %w_mid.3, ...), custom_call_target="tpu_custom_call", output_to_operand_aliasing={{0}: (5, {}), {1}: (6, {}), {2}: (7, {})} | custom-call | flops 20000000 | bytes 8000000 | tf_op jit(solution)/shard_map/update/pallas_call | solution.py:271
  (76 shorter events, 14.1 us)
Async XLA Ops:
  3.0 6.7 %collective-permute-start.1 = (f32[2,16,128]{2,1,0:T(8,128)S(1)}, f32[2,16,128]{2,1,0:T(8,128)S(1)}, u32[]{:S(2)}, u32[]{:S(2)}) collective-permute-start(f32[2,16,128]{2,1,0:T(8,128)S(1)} %bitcast.60), channel_id=1, source_target_pairs={{0,3},{1,0},{2,1},{3,2},{4,7},{5,4},{6,5},{7,6},{8,11},{9,8},{10,9... | collective-permute-start | bytes 49160 | tf_op jit(solution)/shard_map/ppermute | solution.py:29
  4.8 4.8 %collective-permute-start = (f32[2,16,128]{2,1,0:T(8,128)S(1)}, f32[2,16,128]{2,1,0:T(8,128)S(1)}, u32[]{:S(2)}, u32[]{:S(2)}) collective-permute-start(f32[2,16,128]{2,1,0:T(8,128)S(1)} %bitcast.59), channel_id=1, source_target_pairs={{0,1},{1,2},{2,3},{3,0},{4,5},{5,6},{6,7},{7,4},{8,9},{9,10},{10,1... | collective-permute-start | bytes 49160 | tf_op jit(solution)/shard_map/ppermute | solution.py:29
  6.1 5.1 %copy-start.4 = (s32[384,1]{0,1:T(1,128)S(1)}, s32[384,1]{0,1:T(1,128)}, u32[]{:S(2)}) copy-start(s32[384,1]{0,1:T(1,128)} %param.12) | copy-start | bytes 4612
  6.1 6.1 %copy-start.3 = (s32[384]{0:T(512)S(1)}, s32[384]{0:T(512)}, u32[]{:S(2)}) copy-start(s32[384]{0:T(512)} %param.13) | copy-start | bytes 4612
  8.9 3.5 %copy-start.1 = (f32[1024,128]{1,0:T(8,128)S(1)}, f32[1024,128]{1,0:T(8,128)}, u32[]{:S(2)}) copy-start(f32[1024,128]{1,0:T(8,128)} %w_out.3) | copy-start | bytes 1572868
  12.5 13.3 %copy-start = (f32[1024,1024]{1,0:T(8,128)S(1)}, f32[1024,1024]{1,0:T(8,128)}, u32[]{:S(2)}) copy-start(f32[1024,1024]{1,0:T(8,128)} %w_mid.3) | copy-start | bytes 12582916
  12.5 21.7 %collective-permute-start.2 = (f16[129,2,512]{2,1,0:T(2,128)(2,1)}, f16[129,2,512]{2,1,0:T(2,128)(2,1)S(1)}, u32[]{:S(2)}, u32[]{:S(2)}) collective-permute-start(f16[129,2,512]{2,1,0:T(2,128)(2,1)} %get-tuple-element.19), channel_id=1, source_target_pairs={{0,124},{4,0},{8,4},{12,8},{16,12},{20,16},{24,20},{28,24},{32,28}... | collective-permute-start | bytes 792584 | tf_op jit(solution)/shard_map/ppermute | solution.py:29
  25.8 1.7 copy-start.2
  29.2 13.8 %collective-permute-start.3 = (f16[129,2,512]{2,1,0:T(2,128)(2,1)S(1)}, f16[129,2,512]{2,1,0:T(2,128)(2,1)S(1)}, u32[]{:S(2)}, u32[]{:S(2)}) collective-permute-start(f16[129,2,512]{2,1,0:T(2,128)(2,1)S(1)} %get-tuple-element.20), channel_id=1, source_target_pairs={{0,4},{4,8},{8,12},{12,16},{16,20},{20,24},{24,28},{28,32},{32,36}... | collective-permute-start | bytes 792584 | tf_op jit(solution)/shard_map/ppermute | solution.py:29
  76.9 14.7 %collective-permute-start.4 = (bf16[64,88,128]{2,1,0:T(8,128)(2,1)}, bf16[64,88,128]{2,1,0:T(8,128)(2,1)S(1)}, u32[]{:S(2)}, u32[]{:S(2)}) collective-permute-start(bf16[64,88,128]{2,1,0:T(8,128)(2,1)} %get-tuple-element.27), channel_id=1, source_target_pairs={{0,1},{1,0},{2,3},{3,2},{4,5},{5,4},{6,7},{7,6},{8,9},{9,8},{10,11... | collective-permute-start | bytes 4325384 | tf_op jit(solution)/shard_map/ppermute | solution.py:289
  171.9 10.8 %collective-permute-start.5 = (f16[5632,128]{1,0:T(8,128)(2,1)S(1)}, f16[5632,128]{1,0:T(8,128)(2,1)S(1)}, u32[]{:S(2)}, u32[]{:S(2)}) collective-permute-start(f16[5632,128]{1,0:T(8,128)(2,1)S(1)} %bitcast.50), channel_id=1, source_target_pairs={{0,1},{1,0},{2,3},{3,2},{4,5},{5,4},{6,7},{7,6},{8,9},{9,8},{10,11... | collective-permute-start | bytes 4325384 | tf_op jit(solution)/shard_map/ppermute | solution.py:307

commit v3 on v2

--- a/solution.py
+++ b/solution.py
@@ -1,5 +1,4 @@
 import functools
-import math
 
 import jax
 import jax.numpy as jnp
@@ -9,6 +8,7 @@
 from jax.sharding import Mesh
 from jax.sharding import PartitionSpec as P
 
+
 BW = 128
 RATE = 0.5
 TARGET_GAIN = 4.0
@@ -29,38 +29,44 @@
     return lax.ppermute(x, axis, [(i, (i + by) % size) for i in range(size)])
 
 
-def stencil_kernel(diffusion, state, edge_rows, edge_cols, corners, after, even, odd):
+GROUP = 8
+
+
+def stencil_kernel(diffusion, state, edge_rows, edge_cols, corners, after, *held):
     chunk, rows, cols = state.shape
     base = pl.program_id(0) * chunk
     tall, wide = rows + 8, cols + BW
-
-    def diffuse(field, at):
+    fields, beside = held
+
+    def sideways(field):
+        return pltpu.roll(field, 1, 1) + pltpu.roll(field, wide - 1, 1)
+
+    def diffuse(g, at):
         rate = diffusion[base + at]
-        beside = pltpu.roll(field, 1, 0) + pltpu.roll(field, tall - 1, 0)
-        beside = beside + pltpu.roll(field, 1, 1) + pltpu.roll(field, wide - 1, 1)
-        return (1.0 - 4.0 * rate) * field + rate * beside
-
-    def first(at, held):
-        upper = jnp.concatenate([state[at], edge_cols[at]], axis=1)
-        lower = jnp.concatenate([edge_rows[at], corners[at]], axis=1)
-        held[...] = diffuse(jnp.concatenate([upper, lower], axis=0), at)
-
-    def second(at, held):
-        after[at] = diffuse(held[...], at)[:rows, :cols]
-
-    first(0, even)
-
-    def pair(at, carry):
-        first(2 * at + 1, odd)
-        second(2 * at, even)
-        first(jnp.minimum(2 * at + 2, chunk - 1), even)
-        second(2 * at + 1, odd)
+        field = fields[g]
+        around = pltpu.roll(field, 1, 0) + pltpu.roll(field, tall - 1, 0) + beside[g]
+        return (1.0 - 4.0 * rate) * field + rate * around
+
+    def group(index, carry):
+        spots = [(g, index * GROUP + g) for g in range(GROUP)]
+        for g, at in spots:
+            upper = jnp.concatenate([state[at], edge_cols[at]], axis=1)
+            lower = jnp.concatenate([edge_rows[at], corners[at]], axis=1)
+            field = jnp.concatenate([upper, lower], axis=0)
+            fields[g] = field
+            beside[g] = sideways(field)
+        for g, at in spots:
+            fields[g] = diffuse(g, at)
+        for g, at in spots:
+            beside[g] = sideways(fields[g])
+        for g, at in spots:
+            after[at] = diffuse(g, at)[:rows, :cols]
         return carry
 
-    lax.fori_loop(0, chunk // 2, pair, 0, unroll=2)
-
-
-def diffuse_twice(state, diffusion, later):
+    lax.fori_loop(0, chunk // GROUP, group, 0)
+
+
+def exchange(state, later):
     levels, rows, cols = state.shape
     half = jnp.float16
     left = shift(jnp.transpose(state[:, :, cols - 2 :], (2, 1, 0)), LEARN, 1)
@@ -75,25 +81,29 @@
     ends, later = lax.optimization_barrier((ends, later))
     above = shift(ends[0], SIM, 1)
     below = shift(ends[1], SIM, -1)
-    edge_cols = jnp.concatenate([right, jnp.zeros((BW - 4, rows, levels), F32), left])
-    edge_cols = jnp.transpose(edge_cols, (2, 1, 0))
-    gap = jnp.zeros((levels, 4, cols), F32)
-    edge_rows = jnp.concatenate(
-        [below[:levels].astype(F32), gap, above[:levels].astype(F32)], axis=1
-    )
-    row = lax.broadcasted_iota(jnp.int32, (levels, 8, BW), 1)
-    lane = lax.broadcasted_iota(jnp.int32, (levels, 8, BW), 2)
-    corners = jnp.zeros((levels, 8, BW), F32)
-    for at, block in ((0, below), (7, above)):
-        ends = block[levels, 0].astype(F32)
-        for spot, value in ((BW - 1, ends[:levels]), (0, ends[levels : 2 * levels])):
-            corners = jnp.where((row == at) & (lane == spot), value[:, None, None], corners)
-    return stencil_call(state, edge_rows, edge_cols, corners, diffusion), later
+
+    def edges():
+        edge_cols = jnp.concatenate([right, jnp.zeros((BW - 4, rows, levels), F32), left])
+        edge_cols = jnp.transpose(edge_cols, (2, 1, 0))
+        gap = jnp.zeros((levels, 4, cols), F32)
+        edge_rows = jnp.concatenate(
+            [below[:levels].astype(F32), gap, above[:levels].astype(F32)], axis=1
+        )
+        row = lax.broadcasted_iota(jnp.int32, (levels, 8, BW), 1)
+        lane = lax.broadcasted_iota(jnp.int32, (levels, 8, BW), 2)
+        corners = jnp.zeros((levels, 8, BW), F32)
+        for at, block in ((0, below), (7, above)):
+            tips = block[levels, 0].astype(F32)
+            for spot, value in ((BW - 1, tips[:levels]), (0, tips[levels : 2 * levels])):
+                corners = jnp.where((row == at) & (lane == spot), value[:, None, None], corners)
+        return edge_rows, edge_cols, corners
+
+    return edges, later
 
 
 def stencil_call(state, edge_rows, edge_cols, corners, diffusion):
     levels, rows, cols = state.shape
-    chunk = 16
+    chunk = 32
 
     def block(*shape):
         return pl.BlockSpec((chunk,) + shape, lambda i: (i, 0, 0))
@@ -110,7 +120,7 @@
             block(8, BW),
         ],
         out_specs=block(rows, cols),
-        scratch_shapes=[pltpu.VMEM((rows + 8, cols + BW), F32)] * 2,
+        scratch_shapes=[pltpu.VMEM((GROUP, rows + 8, cols + BW), F32)] * 2,
         name="stencil",
     )(diffusion, state, edge_rows, edge_cols, corners)
 
@@ -135,14 +145,73 @@
     target[:, :80], target[:, 80:] = high, low
 
 
-def network_kernel(
-    count, meta, state, after, w1t, w2t, w2, w3t, w3, grads, send, xbuf, abuf, slope1, slope2, sems
-):
+def prepare_kernel(where, tiles, places, w_in, w_mid, w_out, meta, w1t, w2t, w2, w3t, w3, held):
+    w1t[...] = w_in[...].T.astype(BF16)
+    w2t[...] = w_mid[...].T.astype(BF16)
+    w2[...] = w_mid[...].astype(BF16)
+    w3t[...] = w_out[...].T.astype(BF16)
+    w3[...] = w_out[...].astype(BF16)
+    groups = (meta.shape[0] - 2) // 2
+    samples = tiles.shape[0] // groups
+
+    def clear(i, carry):
+        held[i] = 0
+        return carry
+
+    lax.fori_loop(0, held.shape[0], clear, 0)
+
+    def group(g, count):
+        place = -1
+        for k in range(samples):
+            place = jnp.where(tiles[g * samples + k] == where[0], places[g * samples + k], place)
+        spot = jnp.maximum(place, 0)
+        earlier = held[spot]
+        fresh = (place >= 0) & (earlier == 0)
+
+        @pl.when((place >= 0) & (earlier > 0))
+        def _():
+            meta[2 + groups + earlier - 1] = 2
+            held[spot] = 0
+
+        @pl.when(fresh)
+        def _():
+            meta[2 + count] = spot
+            meta[2 + groups + count] = 1
+            held[spot] = count + 1
+
+        return count + fresh.astype(jnp.int32)
+
+    meta[0] = lax.fori_loop(0, groups, group, 0)
+    meta[1] = where[1]
+
+
+def prepare(where, tiles, places, weights, groups, spots):
+    levels, hid = weights[0].shape
+    smem = pl.BlockSpec(memory_space=pltpu.SMEM)
+    vmem = pl.BlockSpec(memory_space=pltpu.VMEM)
+    shapes = ((hid, levels), (hid, hid), (hid, hid), (levels, hid), (hid, levels))
+    return pl.pallas_call(
+        prepare_kernel,
+        out_shape=[jax.ShapeDtypeStruct((2 + 2 * groups,), jnp.int32)]
+        + [jax.ShapeDtypeStruct(shape, BF16) for shape in shapes],
+        in_specs=[smem] * 3 + [vmem] * 3,
+        out_specs=[smem] + [vmem] * 5,
+        scratch_shapes=[pltpu.SMEM((spots,), jnp.int32)],
+        cost_estimate=pl.CostEstimate(flops=20_000_000, bytes_accessed=9_000_000, transcendentals=0),
+        name="prepare",
+    )(where, tiles, places, *weights)
+
+
+def network_kernel(count, meta, state, after, *refs):
+    given, (own, send, grads), kept = refs[:5], refs[5:8], refs[8:13]
+    xbuf, abuf, slope1, slope2, sems, loads, leave = refs[13:]
+    w1t, w2t, w2, w3t, w3 = kept
     total, core = meta[0], meta[1]
     steps = (total + STEP - 1) // STEP
     per_row = state.shape[2] // BW
     levels = w1t.shape[1]
     hid = w2.shape[0]
+    groups = (meta.shape[0] - 2) // 2
 
     def copies(step, slot, i):
         spot = meta[2 + step * STEP + i]
@@ -169,7 +238,13 @@
     def _():
         fetch(0, 0)
 
+    moves = [pltpu.make_async_copy(given[i], kept[i], loads.at[i]) for i in range(5)]
+    for move in moves:
+        move.start()
     grads[...] = jnp.zeros_like(grads)
+    lane = lax.broadcasted_iota(jnp.int32, (1, STEP * BW), 1) // BW
+    for move in moves:
+        move.wait()
 
     def body(step, carry):
         slot = lax.rem(step, 2)
@@ -198,7 +273,13 @@
         act_one, slope1[...] = activate(dot(w1t[...], inputs))
         act_two, slope2[...] = activate(dot(w2t[...], act_one))
         output = dot(w3t[...], act_two)
+        times = jnp.ones((1, STEP * BW), F32)
+        for i in range(STEP):
+            index = step * STEP + i
+            often = jnp.where(index < total, meta[2 + groups + jnp.minimum(index, groups - 1)], 1)
+            times = jnp.where(lane == i, often.astype(F32), times)
         error = ((output - targets.astype(F32)) / count).astype(BF16)
+        error = (error.astype(F32) * times).astype(BF16)
         grads[:, :, :, 72:] += dot_t(act_two, error).reshape(2, 8, 8, 8, BW)
         delta_two = (dot(w3[...], error) * slope2[...]).astype(BF16)
         for j in range(0, hid // BW, 2):
@@ -214,33 +295,39 @@
         return carry
 
     lax.fori_loop(0, steps, body, 0)
+    out = pltpu.make_async_copy(grads.at[core], own, leave)
+    out.start()
     store_split(send, grads[1 - core].reshape(SHARDS, 80, BW))
-
-
-def network(meta, state, after, weight_in, weight_mid, weight_out, count):
-    levels, hid = weight_in.shape
-    first, second, third = (w.astype(BF16) for w in (weight_in, weight_mid, weight_out))
+    out.wait()
+
+
+def network(meta, state, after, ready, count):
+    hid, levels = ready[0].shape
     vmem = pl.BlockSpec(memory_space=pltpu.VMEM)
     hbm = pl.BlockSpec(memory_space=pl.ANY)
     width = STEP * BW
     return pl.pallas_call(
         functools.partial(network_kernel, count),
         out_shape=(
-            jax.ShapeDtypeStruct((2, 8, 8, 80, BW), F32),
+            jax.ShapeDtypeStruct((8, 8, 80, BW), F32),
             jax.ShapeDtypeStruct((SHARDS, 88, BW), BF16),
         ),
-        in_specs=[pl.BlockSpec(memory_space=pltpu.SMEM), hbm, hbm] + [vmem] * 5,
-        out_specs=(vmem, vmem),
-        scratch_shapes=[
+        in_specs=[pl.BlockSpec(memory_space=pltpu.SMEM)] + [hbm] * 7,
+        out_specs=(hbm, vmem),
+        scratch_shapes=[pltpu.VMEM((2, 8, 8, 80, BW), F32)]
+        + [pltpu.VMEM(w.shape, BF16) for w in ready]
+        + [
             pltpu.VMEM((2, levels, width), F32),
             pltpu.VMEM((2, levels, width), F32),
             pltpu.VMEM((hid, width), F32),
             pltpu.VMEM((hid, width), F32),
             pltpu.SemaphoreType.DMA((2, STEP, 2)),
+            pltpu.SemaphoreType.DMA((5,)),
+            pltpu.SemaphoreType.DMA,
         ],
         compiler_params=pltpu.CompilerParams(vmem_limit_bytes=56 * 1024 * 1024),
         name="network",
-    )(meta, state, after, first.T, second.T, second, third.T, third)
+    )(meta, state, after, *ready)
 
 
 def update_kernel(half, total, w_in, w_mid, w_out, *rest):
@@ -283,12 +370,11 @@
     )(half[None], total, *weights, *news)
 
 
-def sum_everywhere(grads, send, weights):
+def sum_everywhere(own, send, weights):
     core = lax.axis_index("c")
     swap = [(0, 1), (1, 0)]
     got = lax.ppermute(send, "c", swap).astype(F32)
-    pair = lax.dynamic_index_in_dim(grads, core, 0, False).reshape(SHARDS, 80, BW)
-    pair = pair + got[:, :80]
+    pair = own.reshape(SHARDS, 80, BW) + got[:, :80]
     last = pair[:, 72:] + got[:, 80:]
     high = lax.reduce_precision(last, 8, 7)
     pair = jnp.concatenate([pair[:, :72], high, last - high], axis=1).astype(BF16)
@@ -315,27 +401,17 @@
 
 
 def on_device(state_field, diffusion, weight_in, weight_mid, weight_out, block_tile, block_pos):
-    levels, tile_rows, tile_cols = state_field.shape
+    senders = lax.axis_size(SIM)
+    samples = block_tile.shape[0] // senders
+    _, tile_rows, tile_cols = state_field.shape
     weights = (weight_in, weight_mid, weight_out)
-    after, late = diffuse_twice(state_field, diffusion, (weights, block_tile, block_pos))
-    late_weights, block_tile, block_pos = late
-    senders = lax.axis_size(SIM)
-    own_index = lax.axis_index(SIM)
-    samples = block_tile.shape[0] // senders
-    tiles = block_tile[:, 0].reshape(senders, samples)
-    places = block_pos.reshape(senders, samples)
-    matched = tiles == own_index
-    place = jnp.sum(jnp.where(matched, places, 0), axis=1)
-    present = jnp.any(matched, axis=1)
-    order = jnp.arange(senders)
-    rank = jnp.sum(jnp.where(order[None, :] < order[:, None], present[None, :], False), axis=1)
-    lands = present[:, None] & (rank[:, None] == order[None, :])
-    slots = jnp.sum(jnp.where(lands, place[:, None], 0), axis=0)
-    total = jnp.sum(present.astype(jnp.int32))
-    meta = jnp.concatenate([jnp.stack([total, lax.axis_index("c")]), slots.astype(jnp.int32)])
+    where = jnp.stack([lax.axis_index(SIM), lax.axis_index("c")]).astype(jnp.int32)
+    edges, late = exchange(state_field, (where, block_tile[:, 0], block_pos))
+    meta, *ready = prepare(*late, weights, senders, tile_rows * tile_cols // BW)
+    after = stencil_call(state_field, *edges(), diffusion)
     count = float(senders * lax.axis_size(LEARN) * samples * BW)
-    grads, send = network(meta, state_field, after, *late_weights, count)
-    new_in, new_mid, new_out = sum_everywhere(grads, send, weights)
+    own, send = network(meta, state_field, after, ready, count)
+    new_in, new_mid, new_out = sum_everywhere(own, send, weights)
     return (after, new_in, new_mid, new_out)
 
 

time: 189 us -> 182 us (0.963)
  starting transfers between devices: 27.4 us -> 16.8 us
  Pallas kernels: 39.3 us -> 49.6 us
  blocking collectives: 77.6 us -> 85.8 us
  other arithmetic: 21.9 us -> 15 us
  local copies, waits for them, and re-layouts: 11.4 us -> 4.99 us
  waiting for transfers between devices: 9.93 us -> 7.25 us
    ppermute x1, starting transfers between devices: 11.7 us -> 0.79 us  [sum_everywhere(): got = lax.ppermute(send, 'c', swap).astype(F32)]
    all_to_all x1, blocking collectives: 7.45 us -> 15.6 us  [sum_everywhere(): held = lax.all_to_all(held, RING, 0, 0, tiled=True)]
    pallas_call x0 -> x1, Pallas kernels: none -> 7.17 us  [prepare(): pl.pallas_call(prepare_kernel, out_shape=[jax.ShapeDtypeStruct((2 + 2 * g...]
    pallas_call x1, Pallas kernels: 17.1 us -> 22.4 us  [network(): pl.pallas_call(functools.partial(network_kernel, count), out_shape=(jax.S...]
    ppermute x4, waiting for transfers between devices: 8.8 us -> 4.19 us  [shift(): return lax.ppermute(x, axis, [(i, (i + by) % size) for i in range(size)])]
    transpose x2 -> x0, local copies, waits for them, and re-layouts: 3.45 us -> none  [network(): return pl.pallas_call(functools.partial(network_kernel, count), out_shape...]
    transpose x3 -> x1, other arithmetic: 3.86 us -> 1.31 us  [edges(): edge_cols = jnp.transpose(edge_cols, (2, 1, 0))]
    convert_element_type x6 -> x4, other arithmetic: 2.83 us -> 0.37 us  [the longest x1 0.18 us: edges(): above[:levels].astype(F32)]
  transfers between devices with their start and end apart: 6 -> 6, of which waited for: 2 -> 2; matrix products, arithmetic and copies ran while one was open for 11% -> 5% of each run, Pallas kernels for 2% -> 6%
where the time goes in v3:
time: 182 us; the launch traced here: 181 us
  blocking collectives  85.8 us (47%)
  Pallas kernels  49.6 us (27%)
  starting transfers between devices  16.8 us (9%)
  other arithmetic  15 us (8%)
  waiting for transfers between devices  7.25 us (4%)
  local copies, waits for them, and re-layouts  4.99 us (3%)
    all_to_all x1, blocking collectives, sum_everywhere(): held = lax.all_to_all(pair.reshape(-1, BW), PLANE, 0, 0, tiled=True)  42.5 us
    all_to_all x2, blocking collectives, sum_everywhere(): sent = lax.all_to_all(spread, axis, 0, 0, tiled=True)  27.8 us
    pallas_call x1, Pallas kernels, network(): pl.pallas_call(functools.partial(network_kernel, count), out_shape=(jax.S...  22.4 us
    all_to_all x1, blocking collectives, sum_everywhere(): held = lax.all_to_all(held, RING, 0, 0, tiled=True)  15.6 us
    ppermute x4, starting transfers between devices, shift(): return lax.ppermute(x, axis, [(i, (i + by) % size) for i in range(size)])  11.4 us
    pallas_call x1, Pallas kernels, stencil_call(): pl.pallas_call(stencil_kernel, out_shape=jax.ShapeDtypeStruct(state.shape...  11.1 us
    pallas_call x2, Pallas kernels, update(): pl.pallas_call(update_kernel, out_shape=[jax.ShapeDtypeStruct(w.shape, F3...  8.89 us
    pallas_call x1, Pallas kernels, prepare(): pl.pallas_call(prepare_kernel, out_shape=[jax.ShapeDtypeStruct((2 + 2 * g...  7.17 us
  transfers between devices with their start and end apart: 6, of which 2 were waited for; matrix products, arithmetic and copies ran while one was open for 5% of the time, Pallas kernels for 6%

profile of v3, /device:TPU:1, one launch (start us, length us, event | category | flops | bytes accessed | tf_op | source)
XLA Modules:
  0.0 181.1 jit_solution(11870398204835473498)
XLA Ops:
  0.6 1.9 %fusion.5 = (f32[128,16,2]{2,1,0:T(8,128)S(1)}, f32[128,16,2]{2,1,0:T(8,128)S(1)}) fusion(f32[128,16,512]{2,1,0:T(8,128)} %state.3), kind=kLoop, calls=%fused_computation.46 | loop fusion | bytes 65536 | tf_op jit(solution)/shard_map/slice | solution.py:72
  3.0 1.4 collective-permute-start.1
  4.8 1.2 collective-permute-start
  6.1 2.8 %convert.48 = f16[128,16,512]{2,1,0:T(8,128)(2,1)S(1)} convert(f32[128,16,512]{2,1,0:T(8,128)} %state.3) | non-fusion elementwise | flops 1048576 | bytes 6291456 | tf_op jit(solution)/shard_map/convert.33
  10.8 0.7 pad_maximum_fusion.2
  11.5 8.7 %collective-permute-start.2 = (f16[129,2,512]{2,1,0:T(2,128)(2,1)S(1)}, f16[129,2,512]{2,1,0:T(2,128)(2,1)S(1)}, u32[]{:S(2)}, u32[]{:S(2)}) collective-permute-start(f16[129,2,512]{2,1,0:T(2,128)(2,1)S(1)} %get-tuple-element.23), channel_id=1, source_target_pairs={{0,124},{4,0},{8,4},{12,8},{16,12},{20,16},{24,20},{28,24},{32,28}... | collective-permute-start | bytes 792584 | tf_op jit(solution)/shard_map/ppermute | solution.py:29
  21.4 7.2 %prepare.1 = (s32[66]{0:T(128)}, bf16[1024,128]{1,0:T(8,128)(2,1)}, bf16[1024,1024]{1,0:T(8,128)(2,1)}, bf16[1024,1024]{1,0:T(8,128)(2,1)}, bf16[128,1024]{1,0:T(8,128)(2,1)}, /*index=5*/bf16[1024,128]{1,0:T(8,128)(2,1)}) custom-call(s32[2]{0:T(128)} %pad_add_fusion.where, s32[384]{0:T(512)} %reduce.1.tiles, s32[384]{0:T(512)} %places, f32[128,1024]{1,0:T(8,128)} %w_in.5, ...), custom_call_target="tpu_custom_call" | custom-call | flops 20000000 | bytes 9000000 | tf_op jit(solution)/shard_map/prepare/pallas_call | solution.py:193
  28.6 1.3 maximum_bitcast_fusion.edge_cols
  29.9 4.2 %collective-permute-done.3 = f16[129,2,512]{2,1,0:T(2,128)(2,1)S(1)} collective-permute-done((f16[129,2,512]{2,1,0:T(2,128)(2,1)S(1)}, f16[129,2,512]{2,1,0:T(2,128)(2,1)S(1)}, u32[]{:S(2)}, u32[]{:S(2)}) %collective-permute-start.3) | collective-permute-done | bytes 264224 | tf_op jit(solution)/shard_map/ppermute | solution.py:29
  34.5 1.8 pad_maximum_fusion.edge_rows
  36.3 1.4 select_select_fusion.corners
  37.7 11.1 %stencil.1.after = f32[128,16,512]{2,1,0:T(8,128)} custom-call(f32[128]{0:T(128)} %diffusion.1, f32[128,16,512]{2,1,0:T(8,128)} %state.3, f32[128,8,512]{2,1,0:T(8,128)} %pad_maximum_fusion.edge_rows, f32[128,16,128]{2,1,0:T(8,128)} %maximum_bitcast_fusion.edge_cols, f32[128,8,128]{2,1,0:T(8,128)} %select_select_fusion.corners), custom_call_target="tpu_custom_call" | custom-call | tf_op jit(solution)/shard_map/stencil/pallas_call | solution.py:111
  48.8 22.4 %network.1 = (f32[8,8,80,128]{3,2,1,0:T(8,128)}, bf16[64,88,128]{2,1,0:T(8,128)(2,1)}) custom-call(s32[66]{0:T(128)} %get-tuple-element.28.meta, f32[128,16,512]{2,1,0:T(8,128)} %state.3, f32[128,16,512]{2,1,0:T(8,128)} %stencil.1.after, bf16[1024,128]{1,0:T(8,128)(2,1)} %get-tuple-element.29.refs_0_, bf16[1024,1024]{1,0:T(8,128)(2,1)} %get-tuple-element.30.refs_1_, ...), custom_call_target="tpu_custom_call" | custom-call | tf_op jit(solution)/shard_map/network/pallas_call | solution.py:309
  71.2 0.8 collective-permute-start.4
  72.0 3.1 %collective-permute-done.4 = bf16[64,88,128]{2,1,0:T(8,128)(2,1)S(1)} collective-permute-done((bf16[64,88,128]{2,1,0:T(8,128)(2,1)}, bf16[64,88,128]{2,1,0:T(8,128)(2,1)S(1)}, u32[]{:S(2)}, u32[]{:S(2)}) %collective-permute-start.4) | collective-permute-done | bytes 1441824 | tf_op jit(solution)/shard_map/ppermute | solution.py:376
  75.9 42.5 %all_to_all.33 = bf16[16,352,128]{2,1,0:T(8,128)(2,1)S(1)} all-to-all(bf16[16,352,128]{2,1,0:T(8,128)(2,1)S(1)} %bitcast.45), channel_id=1, replica_groups=mesh['z'=4,'y'=4,'xh'=2,'xl'=2,'c'=2] {'z','y'}, dimensions={0} | all-to-all | bytes 2883584 | tf_op jit(solution)/shard_map/all_to_all | solution.py:382
  118.6 15.6 %all_to_all.34 = f32[4,88,128]{2,1,0:T(8,128)S(1)} all-to-all(f32[4,88,128]{2,1,0:T(8,128)S(1)} %bitcast.47), channel_id=1, replica_groups=mesh['z'=4,'y'=4,'xh'=2,'xl'=2,'c'=2] {'xh','xl'}, dimensions={0} | all-to-all | bytes 360448 | tf_op jit(solution)/shard_map/all_to_all | solution.py:384
  135.6 7.0 %all_to_all.35 = f16[4,88,128]{2,1,0:T(8,128)(2,1)S(1)} all-to-all(f16[4,88,128]{2,1,0:T(8,128)(2,1)S(1)} %broadcast_in_dim.65), channel_id=1, replica_groups=mesh['z'=4,'y'=4,'xh'=2,'xl'=2,'c'=2] {'xh','xl'}, dimensions={0} | all-to-all | bytes 180224 | tf_op jit(solution)/shard_map/all_to_all | solution.py:392
  142.8 20.8 %all_to_all.36 = f16[16,352,128]{2,1,0:T(8,128)(2,1)S(1)} all-to-all(f16[16,352,128]{2,1,0:T(8,128)(2,1)S(1)} %broadcast_in_dim.66), channel_id=1, replica_groups=mesh['z'=4,'y'=4,'xh'=2,'xl'=2,'c'=2] {'z','y'}, dimensions={0} | all-to-all | bytes 2883584 | tf_op jit(solution)/shard_map/all_to_all | solution.py:392
  163.6 4.6 %collective-permute-start.5 = (f16[5632,128]{1,0:T(8,128)(2,1)S(1)}, f16[5632,128]{1,0:T(8,128)(2,1)S(1)}, u32[]{:S(2)}, u32[]{:S(2)}) collective-permute-start(f16[5632,128]{1,0:T(8,128)(2,1)S(1)} %bitcast.43), channel_id=1, source_target_pairs={{0,1},{1,0},{2,3},{3,2},{4,5},{5,4},{6,7},{7,6},{8,9},{9,8},{10,11... | collective-permute-start | bytes 4325384 | tf_op jit(solution)/shard_map/ppermute | solution.py:393
  168.5 1.8 slice_multiply_fusion
  170.2 4.4 %update.2 = (f32[128,1024]{1,0:T(8,128)}, f32[1024,1024]{1,0:T(8,128)}, f32[1024,128]{1,0:T(8,128)}) custom-call(s32[1]{0:T(128)} %bitcast.9.half, f32[8,8,80,128]{3,2,1,0:T(8,128)} %bitcast.42, f32[128,1024]{1,0:T(8,128)} %w_in.5, f32[1024,1024]{1,0:T(8,128)} %w_mid.5, f32[1024,128]{1,0:T(8,128)} %w_out.5), custom_call_target="tpu_custom_call" | custom-call | flops 20000000 | bytes 8000000 | tf_op jit(solution)/shard_map/update/pallas_call | solution.py:358
  174.9 1.8 slice_multiply_fusion.1
  176.7 4.4 %update.3 = (f32[128,1024]{1,0:T(8,128)}, f32[1024,1024]{1,0:T(8,128)}, f32[1024,128]{1,0:T(8,128)}) custom-call(s32[1]{0:T(128)} %bitcast.15.half, f32[8,8,80,128]{3,2,1,0:T(8,128)} %bitcast.41, f32[128,1024]{1,0:T(8,128)} %w_in.5, f32[1024,1024]{1,0:T(8,128)} %w_mid.5, ...), custom_call_target="tpu_custom_call", output_to_operand_aliasing={{0}: (5, {}), {1}: (6, {}), {2}: (7, {})} | custom-call | flops 20000000 | bytes 8000000 | tf_op jit(solution)/shard_map/update/pallas_call | solution.py:358
  (56 shorter events, 6.6 us)
Async XLA Ops:
  3.0 7.6 %collective-permute-start.1 = (f32[2,16,128]{2,1,0:T(8,128)S(1)}, f32[2,16,128]{2,1,0:T(8,128)S(1)}, u32[]{:S(2)}, u32[]{:S(2)}) collective-permute-start(f32[2,16,128]{2,1,0:T(8,128)S(1)} %bitcast.52), channel_id=1, source_target_pairs={{0,3},{1,0},{2,1},{3,2},{4,7},{5,4},{6,5},{7,6},{8,11},{9,8},{10,9... | collective-permute-start | bytes 49160 | tf_op jit(solution)/shard_map/ppermute | solution.py:29
  4.8 5.8 %collective-permute-start = (f32[2,16,128]{2,1,0:T(8,128)S(1)}, f32[2,16,128]{2,1,0:T(8,128)S(1)}, u32[]{:S(2)}, u32[]{:S(2)}) collective-permute-start(f32[2,16,128]{2,1,0:T(8,128)S(1)} %bitcast.51), channel_id=1, source_target_pairs={{0,1},{1,2},{2,3},{3,0},{4,5},{5,6},{6,7},{7,4},{8,9},{9,10},{10,1... | collective-permute-start | bytes 49160 | tf_op jit(solution)/shard_map/ppermute | solution.py:29
  6.1 3.9 %copy-start.1 = (s32[384,1]{0,1:T(1,128)S(1)}, s32[384,1]{0,1:T(1,128)}, u32[]{:S(2)}) copy-start(s32[384,1]{0,1:T(1,128)} %param.12) | copy-start | bytes 4612
  11.5 18.4 %collective-permute-start.2 = (f16[129,2,512]{2,1,0:T(2,128)(2,1)S(1)}, f16[129,2,512]{2,1,0:T(2,128)(2,1)S(1)}, u32[]{:S(2)}, u32[]{:S(2)}) collective-permute-start(f16[129,2,512]{2,1,0:T(2,128)(2,1)S(1)} %get-tuple-element.23), channel_id=1, source_target_pairs={{0,124},{4,0},{8,4},{12,8},{16,12},{20,16},{24,20},{28,24},{32,28}... | collective-permute-start | bytes 792584 | tf_op jit(solution)/shard_map/ppermute | solution.py:29
  20.3 13.8 %collective-permute-start.3 = (f16[129,2,512]{2,1,0:T(2,128)(2,1)S(1)}, f16[129,2,512]{2,1,0:T(2,128)(2,1)S(1)}, u32[]{:S(2)}, u32[]{:S(2)}) collective-permute-start(f16[129,2,512]{2,1,0:T(2,128)(2,1)S(1)} %get-tuple-element.24), channel_id=1, source_target_pairs={{0,4},{4,8},{8,12},{12,16},{16,20},{20,24},{24,28},{28,32},{32,36}... | collective-permute-start | bytes 792584 | tf_op jit(solution)/shard_map/ppermute | solution.py:29
  71.2 4.1 %copy-start = (f32[8,8,80,128]{3,2,1,0:T(8,128)S(1)}, f32[8,8,80,128]{3,2,1,0:T(8,128)}, u32[]{:S(2)}) copy-start(f32[8,8,80,128]{3,2,1,0:T(8,128)} %get-tuple-element.34) | copy-start | bytes 7864324
  71.2 3.8 %collective-permute-start.4 = (bf16[64,88,128]{2,1,0:T(8,128)(2,1)}, bf16[64,88,128]{2,1,0:T(8,128)(2,1)S(1)}, u32[]{:S(2)}, u32[]{:S(2)}) collective-permute-start(bf16[64,88,128]{2,1,0:T(8,128)(2,1)} %get-tuple-element.35), channel_id=1, source_target_pairs={{0,1},{1,0},{2,3},{3,2},{4,5},{5,4},{6,7},{7,6},{8,9},{9,8},{10,11... | collective-permute-start | bytes 4325384 | tf_op jit(solution)/shard_map/ppermute | solution.py:376
  163.6 11.1 %collective-permute-start.5 = (f16[5632,128]{1,0:T(8,128)(2,1)S(1)}, f16[5632,128]{1,0:T(8,128)(2,1)S(1)}, u32[]{:S(2)}, u32[]{:S(2)}) collective-permute-start(f16[5632,128]{1,0:T(8,128)(2,1)S(1)} %bitcast.43), channel_id=1, source_target_pairs={{0,1},{1,0},{2,3},{3,2},{4,5},{5,4},{6,7},{7,6},{8,9},{9,8},{10,11... | collective-permute-start | bytes 4325384 | tf_op jit(solution)/shard_map/ppermute | solution.py:393

commit v4 on v3

--- a/solution.py
+++ b/solution.py
@@ -32,11 +32,15 @@
 GROUP = 8
 
 
-def stencil_kernel(diffusion, state, edge_rows, edge_cols, corners, after, *held):
+def stencil_kernel(diffusion, tips, state, below, above, edge_cols, after, *held):
     chunk, rows, cols = state.shape
     base = pl.program_id(0) * chunk
     tall, wide = rows + 8, cols + BW
     fields, beside = held
+    row = lax.broadcasted_iota(jnp.int32, (8, BW), 0)
+    lane = lax.broadcasted_iota(jnp.int32, (8, BW), 1)
+    gap = jnp.zeros((4, cols), F32)
+    ends = [(at, spot) for at in (0, 7) for spot in (BW - 1, 0)]
 
     def sideways(field):
         return pltpu.roll(field, 1, 1) + pltpu.roll(field, wide - 1, 1)
@@ -51,7 +55,11 @@
         spots = [(g, index * GROUP + g) for g in range(GROUP)]
         for g, at in spots:
             upper = jnp.concatenate([state[at], edge_cols[at]], axis=1)
-            lower = jnp.concatenate([edge_rows[at], corners[at]], axis=1)
+            corners = jnp.zeros((8, BW), F32)
+            for tip, (end, spot) in enumerate(ends):
+                corners = jnp.where((row == end) & (lane == spot), tips[tip, base + at], corners)
+            lower = jnp.concatenate([below[at], gap, above[at]], axis=0)
+            lower = jnp.concatenate([lower, corners], axis=1)
             field = jnp.concatenate([upper, lower], axis=0)
             fields[g] = field
             beside[g] = sideways(field)
@@ -85,44 +93,33 @@
     def edges():
         edge_cols = jnp.concatenate([right, jnp.zeros((BW - 4, rows, levels), F32), left])
         edge_cols = jnp.transpose(edge_cols, (2, 1, 0))
-        gap = jnp.zeros((levels, 4, cols), F32)
-        edge_rows = jnp.concatenate(
-            [below[:levels].astype(F32), gap, above[:levels].astype(F32)], axis=1
+        below_f32, above_f32 = below.astype(F32), above.astype(F32)
+        tips = jnp.concatenate(
+            [block[levels, 0, : 2 * levels].reshape(2, levels) for block in (below_f32, above_f32)]
         )
-        row = lax.broadcasted_iota(jnp.int32, (levels, 8, BW), 1)
-        lane = lax.broadcasted_iota(jnp.int32, (levels, 8, BW), 2)
-        corners = jnp.zeros((levels, 8, BW), F32)
-        for at, block in ((0, below), (7, above)):
-            tips = block[levels, 0].astype(F32)
-            for spot, value in ((BW - 1, tips[:levels]), (0, tips[levels : 2 * levels])):
-                corners = jnp.where((row == at) & (lane == spot), value[:, None, None], corners)
-        return edge_rows, edge_cols, corners
+        return tips, below_f32, above_f32, edge_cols
 
     return edges, later
 
 
-def stencil_call(state, edge_rows, edge_cols, corners, diffusion):
+def stencil_call(state, tips, below, above, edge_cols, diffusion):
     levels, rows, cols = state.shape
     chunk = 32
 
     def block(*shape):
         return pl.BlockSpec((chunk,) + shape, lambda i: (i, 0, 0))
 
+    smem = pl.BlockSpec(memory_space=pltpu.SMEM)
     return pl.pallas_call(
         stencil_kernel,
         out_shape=jax.ShapeDtypeStruct(state.shape, F32),
         grid=(levels // chunk,),
-        in_specs=[
-            pl.BlockSpec(memory_space=pltpu.SMEM),
-            block(rows, cols),
-            block(8, cols),
-            block(rows, BW),
-            block(8, BW),
-        ],
+        in_specs=[smem, smem, block(rows, cols)]
+        + [block(2, cols), block(2, cols), block(rows, BW)],
         out_specs=block(rows, cols),
         scratch_shapes=[pltpu.VMEM((GROUP, rows + 8, cols + BW), F32)] * 2,
         name="stencil",
-    )(diffusion, state, edge_rows, edge_cols, corners)
+    )(diffusion, tips, state, below, above, edge_cols)
 
 
 def dot(a, b):
@@ -330,44 +327,36 @@
     )(meta, state, after, *ready)
 
 
-def update_kernel(half, total, w_in, w_mid, w_out, *rest):
-    new_in, new_mid, new_out = rest[-3:]
-    for a in range(total.shape[0]):
-        for b in range(8):
-            step = RATE * total[a, b]
-            lanes = slice(b * BW, (b + 1) * BW)
-            rows = slice(a * 8, (a + 1) * 8)
-            new_in[rows, lanes] = w_in[rows, lanes] - step[64:72]
-            rows = slice(a * 64 + b * 8, a * 64 + (b + 1) * 8)
-            new_out[rows, :] = w_out[rows, :] - step[72:]
-            for j in range(8):
-                lanes = slice(j * BW, (j + 1) * BW)
-                new_mid[rows, lanes] = w_mid[rows, lanes] - step[j * 8 : (j + 1) * 8]
-
-
-def update(half, total, weights, news):
-    hid = weights[1].shape[0]
-    a = 2
-    steps = 8 // a
-    blocks = [
-        pl.BlockSpec((8 * a, hid), lambda i, half: (half[0] * steps + i, 0)),
-        pl.BlockSpec((64 * a, hid), lambda i, half: (half[0] * steps + i, 0)),
-        pl.BlockSpec((64 * a, BW), lambda i, half: (half[0] * steps + i, 0)),
-    ]
-    kept = [pl.BlockSpec(memory_space=pl.ANY)] * len(news)
+def update_kernel(core, mine, theirs, w_in, w_mid, w_out, new_in, new_mid, new_out):
+    for total, half in ((mine, core[0]), (theirs, 1 - core[0])):
+
+        def part(a, carry, total=total, half=half):
+            block = half * 8 + a
+            for b in range(8):
+                step = RATE * total[a, b]
+                lanes = slice(b * BW, (b + 1) * BW)
+                rows = pl.ds(pl.multiple_of(block * 8, 8), 8)
+                new_in[rows, lanes] = w_in[rows, lanes] - step[64:72]
+                rows = pl.ds(pl.multiple_of(block * 64 + b * 8, 8), 8)
+                new_out[rows, :] = w_out[rows, :] - step[72:]
+                for j in range(8):
+                    lanes = slice(j * BW, (j + 1) * BW)
+                    new_mid[rows, lanes] = w_mid[rows, lanes] - step[j * 8 : (j + 1) * 8]
+            return carry
+
+        lax.fori_loop(0, 8, part, 0)
+
+
+def update(core, mine, theirs, weights):
+    vmem = pl.BlockSpec(memory_space=pltpu.VMEM)
     return pl.pallas_call(
         update_kernel,
         out_shape=[jax.ShapeDtypeStruct(w.shape, F32) for w in weights],
-        grid_spec=pltpu.PrefetchScalarGridSpec(
-            num_scalar_prefetch=1,
-            grid=(steps,),
-            in_specs=[pl.BlockSpec((a, 8, 80, BW), lambda i, half: (i, 0, 0, 0))] + blocks + kept,
-            out_specs=blocks,
-        ),
-        input_output_aliases={5 + i: i for i in range(len(news))},
-        cost_estimate=pl.CostEstimate(flops=20_000_000, bytes_accessed=8_000_000, transcendentals=0),
+        in_specs=[pl.BlockSpec(memory_space=pltpu.SMEM)] + [vmem] * 5,
+        out_specs=[vmem] * 3,
+        compiler_params=pltpu.CompilerParams(vmem_limit_bytes=24 * 1024 * 1024),
         name="update",
-    )(half[None], total, *weights, *news)
+    )(core[None], mine, theirs, *weights)
 
 
 def sum_everywhere(own, send, weights):
@@ -381,23 +370,24 @@
     ring, plane = lax.axis_size(RING), lax.axis_size(PLANE)
     held = lax.all_to_all(pair.reshape(-1, BW), PLANE, 0, 0, tiled=True)
     held = jnp.sum(held.reshape(plane, -1, BW).astype(F32), axis=0)
+    held = held.reshape(ring, 88, BW)
+    held = jnp.concatenate([held[:, :72], held[:, 72:80] + held[:, 80:]], axis=1).reshape(-1, BW)
+    rows = held.shape[0]
+    held = jnp.broadcast_to(held, (ring, rows, BW)).reshape(-1, BW)
     held = lax.all_to_all(held, RING, 0, 0, tiled=True)
-    held = jnp.sum(held.reshape(ring, -1, BW), axis=0)
-    held = jnp.concatenate([held[:72], held[72:80] + held[80:]])
+    held = jnp.sum(held.reshape(ring, rows, BW), axis=0)
     power = jnp.floor(jnp.log2(jnp.maximum(jnp.max(jnp.abs(held)), 1e-30)))
     sent = (held * jnp.exp2(14.0 - power)).astype(jnp.float16)
     sent = jnp.concatenate([sent, jnp.full((8, BW), power, jnp.float16)])
-    for axis, size in ((RING, ring), (PLANE, plane)):
-        spread = jnp.broadcast_to(sent, (size,) + sent.shape).reshape(-1, BW)
-        sent = lax.all_to_all(spread, axis, 0, 0, tiled=True)
+    sent = jnp.broadcast_to(sent, (plane, rows + 8, BW)).reshape(-1, BW)
+    sent = lax.all_to_all(sent, PLANE, 0, 0, tiled=True)
     away = lax.ppermute(sent, "c", swap)
 
     def opened(block):
-        block = block.reshape(SHARDS, 88, BW).astype(F32)
-        return (block[:, :80] * jnp.exp2(block[:, 80:81] - 14.0)).reshape(8, 8, 80, BW)
-
-    news = update(core, opened(sent), weights, ())
-    return update(1 - core, opened(away), weights, news)
+        block = block.reshape(plane, rows + 8, BW).astype(F32)
+        return (block[:, :rows] * jnp.exp2(block[:, rows : rows + 1] - 14.0)).reshape(8, 8, 80, BW)
+
+    return update(core, opened(sent), opened(away), weights)
 
 
 def on_device(state_field, diffusion, weight_in, weight_mid, weight_out, block_tile, block_pos):

time: 182 us -> 171 us (0.940)
  Pallas kernels: 49.6 us -> 43.8 us
  other arithmetic: 15 us -> 9.44 us
  local copies, waits for them, and re-layouts: 4.99 us -> 7.23 us
  waiting for transfers between devices: 7.25 us -> 9.2 us
    all_to_all x2 -> x1, blocking collectives: 27.8 us -> 21.7 us  [sum_everywhere(): sent = lax.all_to_all(sent, PLANE, 0, 0, tiled=True)]
    pallas_call x2 -> x1, Pallas kernels: 8.89 us -> 3.12 us  [update(): pl.pallas_call(update_kernel, out_shape=[jax.ShapeDtypeStruct(w.shape, F3...]
    all_to_all x1, blocking collectives: 15.6 us -> 19.6 us  [sum_everywhere(): held = lax.all_to_all(held, RING, 0, 0, tiled=True)]
    mul x2, other arithmetic: 3.51 us -> 0.55 us  [opened(): block[:, :rows] * jnp.exp2(block[:, rows:rows + 1] - 14.0)]
    unnamed x6 -> x16, local copies, waits for them, and re-layouts: 0.88 us -> 3.18 us
    ppermute x1, waiting for transfers between devices: 0.01 us -> 2.22 us  [sum_everywhere(): away = lax.ppermute(sent, 'c', swap)]
  transfers between devices with their start and end apart: 6 -> 6, of which waited for: 2 -> 3; matrix products, arithmetic and copies ran while one was open for 5% -> 5% of each run, Pallas kernels for 6% -> 4%
where the time goes in v4:
time: 171 us
  blocking collectives  84 us (49%)
  Pallas kernels  43.8 us (26%)
  starting transfers between devices  15.7 us (9%)
  other arithmetic  9.44 us (6%)
  waiting for transfers between devices  9.2 us (5%)
  local copies, waits for them, and re-layouts  7.23 us (4%)
  between operations  1.74 us (1%)
    all_to_all x1, blocking collectives, sum_everywhere(): held = lax.all_to_all(pair.reshape(-1, BW), PLANE, 0, 0, tiled=True)  42.6 us
    pallas_call x1, Pallas kernels, network(): pl.pallas_call(functools.partial(network_kernel, count), out_shape=(jax.S...  22.4 us
    all_to_all x1, blocking collectives, sum_everywhere(): sent = lax.all_to_all(sent, PLANE, 0, 0, tiled=True)  21.7 us
    all_to_all x1, blocking collectives, sum_everywhere(): held = lax.all_to_all(held, RING, 0, 0, tiled=True)  19.6 us
    ppermute x4, starting transfers between devices, shift(): return lax.ppermute(x, axis, [(i, (i + by) % size) for i in range(size)])  11.4 us
    pallas_call x1, Pallas kernels, stencil_call(): pl.pallas_call(stencil_kernel, out_shape=jax.ShapeDtypeStruct(state.shape...  11.2 us
    pallas_call x1, Pallas kernels, prepare(): pl.pallas_call(prepare_kernel, out_shape=[jax.ShapeDtypeStruct((2 + 2 * g...  7.18 us
    ppermute x4, waiting for transfers between devices, shift(): return lax.ppermute(x, axis, [(i, (i + by) % size) for i in range(size)])  3.92 us
  transfers between devices with their start and end apart: 6, of which 3 were waited for; matrix products, arithmetic and copies ran while one was open for 5% of the time, Pallas kernels for 4%

profile of v4, /device:TPU:1, one launch (start us, length us, event | category | flops | bytes accessed | tf_op | source)
XLA Modules:
  0.0 171.1 jit_solution(16557094507580383430)
XLA Ops:
  0.6 1.9 %fusion.5 = (f32[128,16,2]{2,1,0:T(8,128)S(1)}, f32[128,16,2]{2,1,0:T(8,128)S(1)}) fusion(f32[128,16,512]{2,1,0:T(8,128)} %state.3), kind=kLoop, calls=%fused_computation.33 | loop fusion | bytes 65536 | tf_op jit(solution)/shard_map/slice | solution.py:80
  3.0 1.4 collective-permute-start.1
  4.8 1.2 collective-permute-start
  6.1 2.8 %convert.47 = f16[128,16,512]{2,1,0:T(8,128)(2,1)S(1)} convert(f32[128,16,512]{2,1,0:T(8,128)} %state.3) | non-fusion elementwise | flops 1048576 | bytes 6291456 | tf_op jit(solution)/shard_map/convert.32
  9.4 0.6 pad_add_fusion.where
  10.0 0.6 reduce.1.tiles
  10.8 0.7 pad_maximum_fusion.1
  11.5 8.7 %collective-permute-start.2 = (f16[129,2,512]{2,1,0:T(2,128)(2,1)S(1)}, f16[129,2,512]{2,1,0:T(2,128)(2,1)S(1)}, u32[]{:S(2)}, u32[]{:S(2)}) collective-permute-start(f16[129,2,512]{2,1,0:T(2,128)(2,1)S(1)} %get-tuple-element.20), channel_id=1, source_target_pairs={{0,124},{4,0},{8,4},{12,8},{16,12},{20,16},{24,20},{28,24},{32,28}... | collective-permute-start | bytes 792584 | tf_op jit(solution)/shard_map/ppermute | solution.py:29
  21.3 7.2 %prepare.1 = (s32[66]{0:T(128)}, bf16[1024,128]{1,0:T(8,128)(2,1)}, bf16[1024,1024]{1,0:T(8,128)(2,1)}, bf16[1024,1024]{1,0:T(8,128)(2,1)}, bf16[128,1024]{1,0:T(8,128)(2,1)}, /*index=5*/bf16[1024,128]{1,0:T(8,128)(2,1)}) custom-call(s32[2]{0:T(128)} %pad_add_fusion.where, s32[384]{0:T(512)} %reduce.1.tiles, s32[384]{0:T(512)} %places, f32[128,1024]{1,0:T(8,128)} %w_in.3, ...), custom_call_target="tpu_custom_call" | custom-call | flops 20000000 | bytes 9000000 | tf_op jit(solution)/shard_map/prepare/pallas_call | solution.py:190
  28.5 1.3 maximum_bitcast_fusion.edge_cols
  30.0 3.9 %collective-permute-done.3 = f16[129,2,512]{2,1,0:T(2,128)(2,1)S(1)} collective-permute-done((f16[129,2,512]{2,1,0:T(2,128)(2,1)S(1)}, f16[129,2,512]{2,1,0:T(2,128)(2,1)S(1)}, u32[]{:S(2)}, u32[]{:S(2)}) %collective-permute-start.3) | collective-permute-done | bytes 264224 | tf_op jit(solution)/shard_map/ppermute | solution.py:29
  34.1 0.6 pad_maximum_fusion.4.tips
  34.9 11.2 %stencil.1.after = f32[128,16,512]{2,1,0:T(8,128)} custom-call(f32[128]{0:T(128)} %diffusion.1, f32[4,128]{1,0:T(4,128)} %pad_maximum_fusion.4.tips, f32[128,16,512]{2,1,0:T(8,128)} %state.3, f32[129,2,512]{2,1,0:T(2,128)} %copy-done.4, f32[129,2,512]{2,1,0:T(2,128)} %copy-done.5, f32[128,16,128]{2,1,0:T(8,128)} %maximum_bitcast_fusion.edge_cols), custom_call_target="tpu_custom_call" | custom-call | tf_op jit(solution)/shard_map/stencil/pallas_call | solution.py:113
  46.1 22.4 %network.1 = (f32[8,8,80,128]{3,2,1,0:T(8,128)}, bf16[64,88,128]{2,1,0:T(8,128)(2,1)}) custom-call(s32[66]{0:T(128)} %get-tuple-element.25.meta, f32[128,16,512]{2,1,0:T(8,128)} %state.3, f32[128,16,512]{2,1,0:T(8,128)} %stencil.1.after, bf16[1024,128]{1,0:T(8,128)(2,1)} %get-tuple-element.26.refs_0_, bf16[1024,1024]{1,0:T(8,128)(2,1)} %get-tuple-element.27.refs_1_, ...), custom_call_target="tpu_custom_call" | custom-call | tf_op jit(solution)/shard_map/network/pallas_call | solution.py:306
  68.5 0.8 collective-permute-start.4
  69.3 3.1 %collective-permute-done.4 = bf16[64,88,128]{2,1,0:T(8,128)(2,1)S(1)} collective-permute-done((bf16[64,88,128]{2,1,0:T(8,128)(2,1)}, bf16[64,88,128]{2,1,0:T(8,128)(2,1)S(1)}, u32[]{:S(2)}, u32[]{:S(2)}) %collective-permute-start.4) | collective-permute-done | bytes 1441824 | tf_op jit(solution)/shard_map/ppermute | solution.py:365
  73.2 42.6 %all_to_all.21 = bf16[16,352,128]{2,1,0:T(8,128)(2,1)S(1)} all-to-all(bf16[16,352,128]{2,1,0:T(8,128)(2,1)S(1)} %bitcast.34), channel_id=1, replica_groups=mesh['z'=4,'y'=4,'xh'=2,'xl'=2,'c'=2] {'z','y'}, dimensions={0} | all-to-all | bytes 2883584 | tf_op jit(solution)/shard_map/all_to_all | solution.py:371
  116.1 19.6 %all_to_all.22 = f32[4,320,128]{2,1,0:T(8,128)S(1)} all-to-all(f32[4,320,128]{2,1,0:T(8,128)S(1)} %broadcast_in_dim.22), channel_id=1, replica_groups=mesh['z'=4,'y'=4,'xh'=2,'xl'=2,'c'=2] {'xh','xl'}, dimensions={0} | all-to-all | bytes 1310720 | tf_op jit(solution)/shard_map/all_to_all | solution.py:377
  135.8 0.6 abs_reduce_fusion
  137.4 21.7 %all_to_all.23 = f16[16,328,128]{2,1,0:T(8,128)(2,1)S(1)} all-to-all(f16[16,328,128]{2,1,0:T(8,128)(2,1)S(1)} %broadcast_in_dim.23), channel_id=1, replica_groups=mesh['z'=4,'y'=4,'xh'=2,'xl'=2,'c'=2] {'z','y'}, dimensions={0} | all-to-all | bytes 2686976 | tf_op jit(solution)/shard_map/all_to_all | solution.py:383
  159.1 3.5 %collective-permute-start.5 = (f16[5248,128]{1,0:T(8,128)(2,1)S(1)}, f16[5248,128]{1,0:T(8,128)(2,1)S(1)}, u32[]{:S(2)}, u32[]{:S(2)}) collective-permute-start(f16[5248,128]{1,0:T(8,128)(2,1)S(1)} %bitcast.35), channel_id=1, source_target_pairs={{0,1},{1,0},{2,3},{3,2},{4,5},{5,4},{6,7},{7,6},{8,9},{9,8},{10,11... | collective-permute-start | bytes 4030472 | tf_op jit(solution)/shard_map/ppermute | solution.py:384
  163.1 2.2 %collective-permute-done.5 = f16[5248,128]{1,0:T(8,128)(2,1)S(1)} collective-permute-done((f16[5248,128]{1,0:T(8,128)(2,1)S(1)}, f16[5248,128]{1,0:T(8,128)(2,1)S(1)}, u32[]{:S(2)}, u32[]{:S(2)}) %collective-permute-start.5) | collective-permute-done | bytes 1343520 | tf_op jit(solution)/shard_map/ppermute | solution.py:384
  165.9 1.9 %copy-done = f32[1024,1024]{1,0:T(8,128)S(1)} copy-done((f32[1024,1024]{1,0:T(8,128)S(1)}, f32[1024,1024]{1,0:T(8,128)}, u32[]{:S(2)}) %copy-start) | copy-done | bytes 4194328
  168.0 3.1 %update.1 = (f32[128,1024]{1,0:T(8,128)}, f32[1024,1024]{1,0:T(8,128)}, f32[1024,128]{1,0:T(8,128)}) custom-call(s32[1]{0:T(128)} %bitcast.9.core, f32[8,8,80,128]{3,2,1,0:T(8,128)S(1)} %bitcast.32, f32[8,8,80,128]{3,2,1,0:T(8,128)S(1)} %bitcast.33, f32[128,1024]{1,0:T(8,128)S(1)} %copy-done.1, f32[1024,1024]{1,0:T(8,128)S(1)} %copy-done, ...), custom_call_target="tpu_custom_call" | custom-call | tf_op jit(solution)/shard_map/update/pallas_call | solution.py:352
  (58 shorter events, 5.7 us)
Async XLA Ops:
  3.0 7.6 %collective-permute-start.1 = (f32[2,16,128]{2,1,0:T(8,128)S(1)}, f32[2,16,128]{2,1,0:T(8,128)S(1)}, u32[]{:S(2)}, u32[]{:S(2)}) collective-permute-start(f32[2,16,128]{2,1,0:T(8,128)S(1)} %bitcast.43), channel_id=1, source_target_pairs={{0,3},{1,0},{2,1},{3,2},{4,7},{5,4},{6,5},{7,6},{8,11},{9,8},{10,9... | collective-permute-start | bytes 49160 | tf_op jit(solution)/shard_map/ppermute | solution.py:29
  4.8 5.8 %collective-permute-start = (f32[2,16,128]{2,1,0:T(8,128)S(1)}, f32[2,16,128]{2,1,0:T(8,128)S(1)}, u32[]{:S(2)}, u32[]{:S(2)}) collective-permute-start(f32[2,16,128]{2,1,0:T(8,128)S(1)} %bitcast.42), channel_id=1, source_target_pairs={{0,1},{1,2},{2,3},{3,0},{4,5},{5,6},{6,7},{7,4},{8,9},{9,10},{10,1... | collective-permute-start | bytes 49160 | tf_op jit(solution)/shard_map/ppermute | solution.py:29
  6.1 3.9 %copy-start.6 = (s32[384,1]{0,1:T(1,128)S(1)}, s32[384,1]{0,1:T(1,128)}, u32[]{:S(2)}) copy-start(s32[384,1]{0,1:T(1,128)} %param.12) | copy-start | bytes 4612
  11.5 18.3 %collective-permute-start.2 = (f16[129,2,512]{2,1,0:T(2,128)(2,1)S(1)}, f16[129,2,512]{2,1,0:T(2,128)(2,1)S(1)}, u32[]{:S(2)}, u32[]{:S(2)}) collective-permute-start(f16[129,2,512]{2,1,0:T(2,128)(2,1)S(1)} %get-tuple-element.20), channel_id=1, source_target_pairs={{0,124},{4,0},{8,4},{12,8},{16,12},{20,16},{24,20},{28,24},{32,28}... | collective-permute-start | bytes 792584 | tf_op jit(solution)/shard_map/ppermute | solution.py:29
  20.2 13.8 %collective-permute-start.3 = (f16[129,2,512]{2,1,0:T(2,128)(2,1)S(1)}, f16[129,2,512]{2,1,0:T(2,128)(2,1)S(1)}, u32[]{:S(2)}, u32[]{:S(2)}) collective-permute-start(f16[129,2,512]{2,1,0:T(2,128)(2,1)S(1)} %get-tuple-element.21), channel_id=1, source_target_pairs={{0,4},{4,8},{8,12},{12,16},{16,20},{20,24},{24,28},{28,32},{32,36}... | collective-permute-start | bytes 792584 | tf_op jit(solution)/shard_map/ppermute | solution.py:29
  30.0 4.8 %copy-start.4 = (f32[129,2,512]{2,1,0:T(2,128)}, f32[129,2,512]{2,1,0:T(2,128)S(1)}, u32[]{:S(2)}) copy-start(f32[129,2,512]{2,1,0:T(2,128)S(1)} %convert_element_type.35.below) | copy-start | bytes 1585156
  34.1 0.8 copy-start.5
  68.5 4.1 %copy-start.3 = (f32[8,8,80,128]{3,2,1,0:T(8,128)S(1)}, f32[8,8,80,128]{3,2,1,0:T(8,128)}, u32[]{:S(2)}) copy-start(f32[8,8,80,128]{3,2,1,0:T(8,128)} %get-tuple-element.31) | copy-start | bytes 7864324
  68.5 3.9 %collective-permute-start.4 = (bf16[64,88,128]{2,1,0:T(8,128)(2,1)}, bf16[64,88,128]{2,1,0:T(8,128)(2,1)S(1)}, u32[]{:S(2)}, u32[]{:S(2)}) collective-permute-start(bf16[64,88,128]{2,1,0:T(8,128)(2,1)} %get-tuple-element.32), channel_id=1, source_target_pairs={{0,1},{1,0},{2,3},{3,2},{4,5},{5,4},{6,7},{7,6},{8,9},{9,8},{10,11... | collective-permute-start | bytes 4325384 | tf_op jit(solution)/shard_map/ppermute | solution.py:365
  159.1 6.2 %collective-permute-start.5 = (f16[5248,128]{1,0:T(8,128)(2,1)S(1)}, f16[5248,128]{1,0:T(8,128)(2,1)S(1)}, u32[]{:S(2)}, u32[]{:S(2)}) collective-permute-start(f16[5248,128]{1,0:T(8,128)(2,1)S(1)} %bitcast.35), channel_id=1, source_target_pairs={{0,1},{1,0},{2,3},{3,2},{4,5},{5,4},{6,7},{7,6},{8,9},{9,8},{10,11... | collective-permute-start | bytes 4030472 | tf_op jit(solution)/shard_map/ppermute | solution.py:384
  165.6 2.2 %copy-start = (f32[1024,1024]{1,0:T(8,128)S(1)}, f32[1024,1024]{1,0:T(8,128)}, u32[]{:S(2)}) copy-start(f32[1024,1024]{1,0:T(8,128)} %w_mid.3) | copy-start | bytes 12582916
  165.6 2.3 %copy-start.1 = (f32[128,1024]{1,0:T(8,128)S(1)}, f32[128,1024]{1,0:T(8,128)}, u32[]{:S(2)}) copy-start(f32[128,1024]{1,0:T(8,128)} %w_in.3) | copy-start | bytes 1572868
  165.6 2.4 %copy-start.2 = (f32[1024,128]{1,0:T(8,128)S(1)}, f32[1024,128]{1,0:T(8,128)}, u32[]{:S(2)}) copy-start(f32[1024,128]{1,0:T(8,128)} %w_out.3) | copy-start | bytes 1572868

commit v5 on v4

--- a/solution.py
+++ b/solution.py
@@ -74,7 +74,7 @@
     lax.fori_loop(0, chunk // GROUP, group, 0)
 
 
-def exchange(state, later):
+def exchange(state):
     levels, rows, cols = state.shape
     half = jnp.float16
     left = shift(jnp.transpose(state[:, :, cols - 2 :], (2, 1, 0)), LEARN, 1)
@@ -86,7 +86,6 @@
         return jnp.concatenate([state[:, first : first + 2], ends]).astype(half)
 
     ends = (outgoing(rows - 2, rows - 1), outgoing(0, 0))
-    ends, later = lax.optimization_barrier((ends, later))
     above = shift(ends[0], SIM, 1)
     below = shift(ends[1], SIM, -1)
 
@@ -99,7 +98,7 @@
         )
         return tips, below_f32, above_f32, edge_cols
 
-    return edges, later
+    return edges
 
 
 def stencil_call(state, tips, below, above, edge_cols, diffusion):
@@ -167,8 +166,8 @@
 
         @pl.when((place >= 0) & (earlier > 0))
         def _():
-            meta[2 + groups + earlier - 1] = 2
-            held[spot] = 0
+            at = 2 + groups + earlier - 1
+            meta[at] = meta[at] + 1
 
         @pl.when(fresh)
         def _():
@@ -327,24 +326,43 @@
     )(meta, state, after, *ready)
 
 
-def update_kernel(core, mine, theirs, w_in, w_mid, w_out, new_in, new_mid, new_out):
-    for total, half in ((mine, core[0]), (theirs, 1 - core[0])):
-
-        def part(a, carry, total=total, half=half):
-            block = half * 8 + a
-            for b in range(8):
-                step = RATE * total[a, b]
-                lanes = slice(b * BW, (b + 1) * BW)
-                rows = pl.ds(pl.multiple_of(block * 8, 8), 8)
-                new_in[rows, lanes] = w_in[rows, lanes] - step[64:72]
-                rows = pl.ds(pl.multiple_of(block * 64 + b * 8, 8), 8)
-                new_out[rows, :] = w_out[rows, :] - step[72:]
-                for j in range(8):
-                    lanes = slice(j * BW, (j + 1) * BW)
-                    new_mid[rows, lanes] = w_mid[rows, lanes] - step[j * 8 : (j + 1) * 8]
-            return carry
-
-        lax.fori_loop(0, 8, part, 0)
+PIECES = 2
+
+
+def update_kernel(core, mine, theirs, *refs):
+    weights, news, held, stores = refs[:3], refs[3:6], refs[6:9], refs[9]
+    span = 8 // PIECES
+    moves = []
+    for order, (total, half) in enumerate(((mine, core[0]), (theirs, 1 - core[0]))):
+        for piece in range(PIECES):
+
+            def rows_of(i, first, count, half=half, piece=piece):
+                size = weights[i].shape[0] // (2 * PIECES)
+                start = (half * PIECES + piece) * size + first
+                return pl.ds(pl.multiple_of(start, 8), count)
+
+            for a in range(span):
+                for b in range(8):
+                    step = RATE * total[piece * span + a, b]
+                    lanes = slice(b * BW, (b + 1) * BW)
+                    old = weights[0][rows_of(0, a * 8, 8), lanes]
+                    held[0][order, piece, a * 8 : (a + 1) * 8, lanes] = old - step[64:72]
+                    at = a * 64 + b * 8
+                    old = weights[2][rows_of(2, at, 8), :]
+                    held[2][order, piece, at : at + 8] = old - step[72:]
+                    for j in range(8):
+                        lanes = slice(j * BW, (j + 1) * BW)
+                        old = weights[1][rows_of(1, at, 8), lanes]
+                        held[1][order, piece, at : at + 8, lanes] = old - step[j * 8 : (j + 1) * 8]
+            for i in range(3):
+                target = news[i].at[rows_of(i, 0, held[i].shape[2])]
+                move = pltpu.make_async_copy(
+                    held[i].at[order, piece], target, stores.at[order * PIECES + piece, i]
+                )
+                move.start()
+                moves.append(move)
+    for move in moves:
+        move.wait()
 
 
 def update(core, mine, theirs, weights):
@@ -353,7 +371,11 @@
         update_kernel,
         out_shape=[jax.ShapeDtypeStruct(w.shape, F32) for w in weights],
         in_specs=[pl.BlockSpec(memory_space=pltpu.SMEM)] + [vmem] * 5,
-        out_specs=[vmem] * 3,
+        out_specs=[pl.BlockSpec(memory_space=pl.ANY)] * 3,
+        scratch_shapes=[
+            pltpu.VMEM((2, PIECES, w.shape[0] // (2 * PIECES), w.shape[1]), F32) for w in weights
+        ]
+        + [pltpu.SemaphoreType.DMA((2 * PIECES, 3))],
         compiler_params=pltpu.CompilerParams(vmem_limit_bytes=24 * 1024 * 1024),
         name="update",
     )(core[None], mine, theirs, *weights)
@@ -396,8 +418,9 @@
     _, tile_rows, tile_cols = state_field.shape
     weights = (weight_in, weight_mid, weight_out)
     where = jnp.stack([lax.axis_index(SIM), lax.axis_index("c")]).astype(jnp.int32)
-    edges, late = exchange(state_field, (where, block_tile[:, 0], block_pos))
-    meta, *ready = prepare(*late, weights, senders, tile_rows * tile_cols // BW)
+    edges = exchange(state_field)
+    spots = tile_rows * tile_cols // BW
+    meta, *ready = prepare(where, block_tile[:, 0], block_pos, weights, senders, spots)
     after = stencil_call(state_field, *edges(), diffusion)
     count = float(senders * lax.axis_size(LEARN) * samples * BW)
     own, send = network(meta, state_field, after, ready, count)

time: 171 us -> 167 us (0.977)
  waiting for transfers between devices: 9.2 us -> 5.65 us
    ppermute x4, waiting for transfers between devices: 3.92 us -> 0.01 us  [shift(): return lax.ppermute(x, axis, [(i, (i + by) % size) for i in range(size)])]
    all_to_all x1, blocking collectives: 42.6 us -> 45.7 us  [sum_everywhere(): held = lax.all_to_all(pair.reshape(-1, BW), PLANE, 0, 0, tiled=True)]
    all_to_all x1, blocking collectives: 19.6 us -> 16.7 us  [sum_everywhere(): held = lax.all_to_all(held, RING, 0, 0, tiled=True)]
  transfers between devices with their start and end apart: 6 -> 6, of which waited for: 3 -> 2; matrix products, arithmetic and copies ran while one was open for 5% -> 5% of each run, Pallas kernels for 4% -> 4%
where the time goes in v5:
time: 167 us
  blocking collectives  84.2 us (50%)
  Pallas kernels  43.3 us (26%)
  starting transfers between devices  15.1 us (9%)
  other arithmetic  9.42 us (6%)
  local copies, waits for them, and re-layouts  7.26 us (4%)
  waiting for transfers between devices  5.65 us (3%)
  between operations  1.93 us (1%)
    all_to_all x1, blocking collectives, sum_everywhere(): held = lax.all_to_all(pair.reshape(-1, BW), PLANE, 0, 0, tiled=True)  45.7 us
    pallas_call x1, Pallas kernels, network(): pl.pallas_call(functools.partial(network_kernel, count), out_shape=(jax.S...  22.4 us
    all_to_all x1, blocking collectives, sum_everywhere(): sent = lax.all_to_all(sent, PLANE, 0, 0, tiled=True)  21.8 us
    all_to_all x1, blocking collectives, sum_everywhere(): held = lax.all_to_all(held, RING, 0, 0, tiled=True)  16.7 us
    ppermute x4, starting transfers between devices, shift(): return lax.ppermute(x, axis, [(i, (i + by) % size) for i in range(size)])  11.5 us
    pallas_call x1, Pallas kernels, stencil_call(): pl.pallas_call(stencil_kernel, out_shape=jax.ShapeDtypeStruct(state.shape...  11.2 us
    pallas_call x1, Pallas kernels, prepare(): pl.pallas_call(prepare_kernel, out_shape=[jax.ShapeDtypeStruct((2 + 2 * g...  7.24 us
    ppermute x1, starting transfers between devices, sum_everywhere(): away = lax.ppermute(sent, 'c', swap)  3.52 us
  transfers between devices with their start and end apart: 6, of which 2 were waited for; matrix products, arithmetic and copies ran while one was open for 5% of the time, Pallas kernels for 4%

profile of v5, /device:TPU:1, one launch (start us, length us, event | category | flops | bytes accessed | tf_op | source)
XLA Modules:
  0.0 166.9 jit_solution(2330639804676281300)
XLA Ops:
  0.6 1.9 %fusion.5 = (f32[128,16,2]{2,1,0:T(8,128)S(1)}, f32[128,16,2]{2,1,0:T(8,128)S(1)}) fusion(f32[128,16,512]{2,1,0:T(8,128)} %state.3), kind=kLoop, calls=%fused_computation.33 | loop fusion | bytes 65536 | tf_op jit(solution)/shard_map/slice | solution.py:80
  3.0 1.4 collective-permute-start.1
  4.8 1.3 collective-permute-start
  6.1 2.8 %convert.47 = f16[128,16,512]{2,1,0:T(8,128)(2,1)S(1)} convert(f32[128,16,512]{2,1,0:T(8,128)} %state.3) | non-fusion elementwise | flops 1048576 | bytes 6291456 | tf_op jit(solution)/shard_map/convert.32
  8.8 0.5 fusion.6
  9.9 2.8 %collective-permute-start.3 = (f16[129,2,512]{2,1,0:T(2,128)(2,1)S(1)}, f16[129,2,512]{2,1,0:T(2,128)(2,1)S(1)}, u32[]{:S(2)}, u32[]{:S(2)}) collective-permute-start(f16[129,2,512]{2,1,0:T(2,128)(2,1)S(1)} %pad_maximum_fusion.2), channel_id=1, source_target_pairs={{0,4},{4,8},{8,12},{12,16},{16,20},{20,24},{24,28},{28,32},{32,36}... | collective-permute-start | bytes 792584 | tf_op jit(solution)/shard_map/ppermute | solution.py:29
  13.1 6.0 %collective-permute-start.2 = (f16[129,2,512]{2,1,0:T(2,128)(2,1)S(1)}, f16[129,2,512]{2,1,0:T(2,128)(2,1)S(1)}, u32[]{:S(2)}, u32[]{:S(2)}) collective-permute-start(f16[129,2,512]{2,1,0:T(2,128)(2,1)S(1)} %pad_maximum_fusion.1), channel_id=1, source_target_pairs={{0,124},{4,0},{8,4},{12,8},{16,12},{20,16},{24,20},{28,24},{32,28}... | collective-permute-start | bytes 792584 | tf_op jit(solution)/shard_map/ppermute | solution.py:29
  19.1 0.6 pad_add_fusion.where
  19.7 0.6 reduce.1.tiles
  20.3 7.2 %prepare.1 = (s32[66]{0:T(128)}, bf16[1024,128]{1,0:T(8,128)(2,1)}, bf16[1024,1024]{1,0:T(8,128)(2,1)}, bf16[1024,1024]{1,0:T(8,128)(2,1)}, bf16[128,1024]{1,0:T(8,128)(2,1)}, /*index=5*/bf16[1024,128]{1,0:T(8,128)(2,1)}) custom-call(s32[2]{0:T(128)} %pad_add_fusion.where, s32[384]{0:T(512)} %reduce.1.tiles, s32[384]{0:T(512)} %places.1, ...), custom_call_target="tpu_custom_call" | custom-call | flops 20000000 | bytes 9000000 | tf_op jit(solution)/shard_map/prepare/pallas_call | solution.py:189
  28.1 0.5 copy.17
  28.6 1.3 maximum_bitcast_fusion.edge_cols
  30.4 0.6 pad_maximum_fusion.4.tips
  31.2 11.2 %stencil.1.after = f32[128,16,512]{2,1,0:T(8,128)} custom-call(f32[128]{0:T(128)} %diffusion.1, f32[4,128]{1,0:T(4,128)} %pad_maximum_fusion.4.tips, f32[128,16,512]{2,1,0:T(8,128)} %state.3, f32[129,2,512]{2,1,0:T(2,128)} %copy-done.5, f32[129,2,512]{2,1,0:T(2,128)} %copy-done.4, f32[128,16,128]{2,1,0:T(8,128)} %maximum_bitcast_fusion.edge_cols), custom_call_target="tpu_custom_call" | custom-call | tf_op jit(solution)/shard_map/stencil/pallas_call | solution.py:112
  42.4 22.4 %network.1 = (f32[8,8,80,128]{3,2,1,0:T(8,128)}, bf16[64,88,128]{2,1,0:T(8,128)(2,1)}) custom-call(s32[66]{0:T(128)} %get-tuple-element.15.meta, f32[128,16,512]{2,1,0:T(8,128)} %state.3, f32[128,16,512]{2,1,0:T(8,128)} %stencil.1.after, bf16[1024,128]{1,0:T(8,128)(2,1)} %get-tuple-element.16.refs_0_, bf16[1024,1024]{1,0:T(8,128)(2,1)} %get-tuple-element.17.refs_1_, ...), custom_call_target="tpu_custom_call" | custom-call | tf_op jit(solution)/shard_map/network/pallas_call | solution.py:305
  64.8 3.4 %collective-permute-done.4 = bf16[64,88,128]{2,1,0:T(8,128)(2,1)S(1)} collective-permute-done((bf16[64,88,128]{2,1,0:T(8,128)(2,1)}, bf16[64,88,128]{2,1,0:T(8,128)(2,1)S(1)}, u32[]{:S(2)}, u32[]{:S(2)}) %collective-permute-start.4) | collective-permute-done | bytes 1441824 | tf_op jit(solution)/shard_map/ppermute | solution.py:387
  69.1 45.7 %all_to_all.21 = bf16[16,352,128]{2,1,0:T(8,128)(2,1)S(1)} all-to-all(bf16[16,352,128]{2,1,0:T(8,128)(2,1)S(1)} %bitcast.34), channel_id=1, replica_groups=mesh['z'=4,'y'=4,'xh'=2,'xl'=2,'c'=2] {'z','y'}, dimensions={0} | all-to-all | bytes 2883584 | tf_op jit(solution)/shard_map/all_to_all | solution.py:393
  115.1 16.7 %all_to_all.22 = f32[4,320,128]{2,1,0:T(8,128)S(1)} all-to-all(f32[4,320,128]{2,1,0:T(8,128)S(1)} %broadcast_in_dim.25), channel_id=1, replica_groups=mesh['z'=4,'y'=4,'xh'=2,'xl'=2,'c'=2] {'xh','xl'}, dimensions={0} | all-to-all | bytes 1310720 | tf_op jit(solution)/shard_map/all_to_all | solution.py:399
  131.8 0.6 abs_reduce_fusion
  133.4 21.8 %all_to_all.23 = f16[16,328,128]{2,1,0:T(8,128)(2,1)S(1)} all-to-all(f16[16,328,128]{2,1,0:T(8,128)(2,1)S(1)} %broadcast_in_dim.26), channel_id=1, replica_groups=mesh['z'=4,'y'=4,'xh'=2,'xl'=2,'c'=2] {'z','y'}, dimensions={0} | all-to-all | bytes 2686976 | tf_op jit(solution)/shard_map/all_to_all | solution.py:405
  155.3 3.5 %collective-permute-start.5 = (f16[5248,128]{1,0:T(8,128)(2,1)S(1)}, f16[5248,128]{1,0:T(8,128)(2,1)S(1)}, u32[]{:S(2)}, u32[]{:S(2)}) collective-permute-start(f16[5248,128]{1,0:T(8,128)(2,1)S(1)} %bitcast.35), channel_id=1, source_target_pairs={{0,1},{1,0},{2,3},{3,2},{4,5},{5,4},{6,7},{7,6},{8,9},{9,8},{10,11... | collective-permute-start | bytes 4030472 | tf_op jit(solution)/shard_map/ppermute | solution.py:406
  159.3 2.2 %collective-permute-done.5 = f16[5248,128]{1,0:T(8,128)(2,1)S(1)} collective-permute-done((f16[5248,128]{1,0:T(8,128)(2,1)S(1)}, f16[5248,128]{1,0:T(8,128)(2,1)S(1)}, u32[]{:S(2)}, u32[]{:S(2)}) %collective-permute-start.5) | collective-permute-done | bytes 1343520 | tf_op jit(solution)/shard_map/ppermute | solution.py:406
  162.0 1.9 %copy-done = f32[1024,1024]{1,0:T(8,128)S(1)} copy-done((f32[1024,1024]{1,0:T(8,128)S(1)}, f32[1024,1024]{1,0:T(8,128)}, u32[]{:S(2)}) %copy-start) | copy-done | bytes 4194328
  164.2 2.6 %update.1 = (f32[128,1024]{1,0:T(8,128)}, f32[1024,1024]{1,0:T(8,128)}, f32[1024,128]{1,0:T(8,128)}) custom-call(s32[1]{0:T(128)} %bitcast.11.core, f32[8,8,80,128]{3,2,1,0:T(8,128)S(1)} %bitcast.32, f32[8,8,80,128]{3,2,1,0:T(8,128)S(1)} %bitcast.33, f32[128,1024]{1,0:T(8,128)S(1)} %copy-done.1, f32[1024,1024]{1,0:T(8,128)S(1)} %copy-done, ...), custom_call_target="tpu_custom_call" | custom-call | tf_op jit(solution)/shard_map/update/pallas_call | solution.py:370
  (59 shorter events, 5.4 us)
Async XLA Ops:
  3.0 6.4 %collective-permute-start.1 = (f32[2,16,128]{2,1,0:T(8,128)S(1)}, f32[2,16,128]{2,1,0:T(8,128)S(1)}, u32[]{:S(2)}, u32[]{:S(2)}) collective-permute-start(f32[2,16,128]{2,1,0:T(8,128)S(1)} %bitcast.43), channel_id=1, source_target_pairs={{0,3},{1,0},{2,1},{3,2},{4,7},{5,4},{6,5},{7,6},{8,11},{9,8},{10,9... | collective-permute-start | bytes 49160 | tf_op jit(solution)/shard_map/ppermute | solution.py:29
  4.8 14.9 %copy-start.6 = (s32[384,1]{0,1:T(1,128)S(1)}, s32[384,1]{0,1:T(1,128)}, u32[]{:S(2)}) copy-start(s32[384,1]{0,1:T(1,128)} %param.12) | copy-start | bytes 4612
  4.8 4.6 %collective-permute-start = (f32[2,16,128]{2,1,0:T(8,128)S(1)}, f32[2,16,128]{2,1,0:T(8,128)S(1)}, u32[]{:S(2)}, u32[]{:S(2)}) collective-permute-start(f32[2,16,128]{2,1,0:T(8,128)S(1)} %bitcast.42), channel_id=1, source_target_pairs={{0,1},{1,2},{2,3},{3,0},{4,5},{5,6},{6,7},{7,4},{8,9},{9,10},{10,1... | collective-permute-start | bytes 49160 | tf_op jit(solution)/shard_map/ppermute | solution.py:29
  9.9 20.0 %collective-permute-start.3 = (f16[129,2,512]{2,1,0:T(2,128)(2,1)S(1)}, f16[129,2,512]{2,1,0:T(2,128)(2,1)S(1)}, u32[]{:S(2)}, u32[]{:S(2)}) collective-permute-start(f16[129,2,512]{2,1,0:T(2,128)(2,1)S(1)} %pad_maximum_fusion.2), channel_id=1, source_target_pairs={{0,4},{4,8},{8,12},{12,16},{16,20},{20,24},{24,28},{28,32},{32,36}... | collective-permute-start | bytes 792584 | tf_op jit(solution)/shard_map/ppermute | solution.py:29
  13.1 17.1 %collective-permute-start.2 = (f16[129,2,512]{2,1,0:T(2,128)(2,1)S(1)}, f16[129,2,512]{2,1,0:T(2,128)(2,1)S(1)}, u32[]{:S(2)}, u32[]{:S(2)}) collective-permute-start(f16[129,2,512]{2,1,0:T(2,128)(2,1)S(1)} %pad_maximum_fusion.1), channel_id=1, source_target_pairs={{0,124},{4,0},{8,4},{12,8},{16,12},{20,16},{24,20},{28,24},{32,28}... | collective-permute-start | bytes 792584 | tf_op jit(solution)/shard_map/ppermute | solution.py:29
  30.1 0.9 copy-start.4
  30.4 0.8 copy-start.5
  64.7 3.7 %copy-start.3 = (f32[8,8,80,128]{3,2,1,0:T(8,128)S(1)}, f32[8,8,80,128]{3,2,1,0:T(8,128)}, u32[]{:S(2)}) copy-start(f32[8,8,80,128]{3,2,1,0:T(8,128)} %get-tuple-element.21) | copy-start | bytes 7864324
  64.7 3.5 %collective-permute-start.4 = (bf16[64,88,128]{2,1,0:T(8,128)(2,1)}, bf16[64,88,128]{2,1,0:T(8,128)(2,1)S(1)}, u32[]{:S(2)}, u32[]{:S(2)}) collective-permute-start(bf16[64,88,128]{2,1,0:T(8,128)(2,1)} %get-tuple-element.22), channel_id=1, source_target_pairs={{0,1},{1,0},{2,3},{3,2},{4,5},{5,4},{6,7},{7,6},{8,9},{9,8},{10,11... | collective-permute-start | bytes 4325384 | tf_op jit(solution)/shard_map/ppermute | solution.py:387
  155.3 6.2 %collective-permute-start.5 = (f16[5248,128]{1,0:T(8,128)(2,1)S(1)}, f16[5248,128]{1,0:T(8,128)(2,1)S(1)}, u32[]{:S(2)}, u32[]{:S(2)}) collective-permute-start(f16[5248,128]{1,0:T(8,128)(2,1)S(1)} %bitcast.35), channel_id=1, source_target_pairs={{0,1},{1,0},{2,3},{3,2},{4,5},{5,4},{6,7},{7,6},{8,9},{9,8},{10,11... | collective-permute-start | bytes 4030472 | tf_op jit(solution)/shard_map/ppermute | solution.py:406
  161.7 2.2 %copy-start = (f32[1024,1024]{1,0:T(8,128)S(1)}, f32[1024,1024]{1,0:T(8,128)}, u32[]{:S(2)}) copy-start(f32[1024,1024]{1,0:T(8,128)} %refs_1_.1) | copy-start | bytes 12582916
  161.7 2.3 %copy-start.1 = (f32[128,1024]{1,0:T(8,128)S(1)}, f32[128,1024]{1,0:T(8,128)}, u32[]{:S(2)}) copy-start(f32[128,1024]{1,0:T(8,128)} %refs_0_.1) | copy-start | bytes 1572868
  161.7 2.4 %copy-start.2 = (f32[1024,128]{1,0:T(8,128)S(1)}, f32[1024,128]{1,0:T(8,128)}, u32[]{:S(2)}) copy-start(f32[1024,128]{1,0:T(8,128)} %refs_2_.1) | copy-start | bytes 1572868

commit v6 on v5

--- a/solution.py
+++ b/solution.py
@@ -203,7 +203,7 @@
     xbuf, abuf, slope1, slope2, sems, loads, leave = refs[13:]
     w1t, w2t, w2, w3t, w3 = kept
     total, core = meta[0], meta[1]
-    steps = (total + STEP - 1) // STEP
+    steps = (total + STEP // 2 - 1) // STEP
     per_row = state.shape[2] // BW
     levels = w1t.shape[1]
     hid = w2.shape[0]
@@ -230,26 +230,25 @@
                 for copy in copies(step, slot, i):
                     copy.start()
 
-    @pl.when(steps > 0)
-    def _():
-        fetch(0, 0)
+    fetch(0, 0)
 
     moves = [pltpu.make_async_copy(given[i], kept[i], loads.at[i]) for i in range(5)]
     for move in moves:
         move.start()
     grads[...] = jnp.zeros_like(grads)
-    lane = lax.broadcasted_iota(jnp.int32, (1, STEP * BW), 1) // BW
     for move in moves:
         move.wait()
 
     def body(step, carry):
+        fetch(step + 1, 1 - lax.rem(step, 2))
+        learn(step, STEP)
+        return carry
+
+    def learn(step, blocks):
         slot = lax.rem(step, 2)
-
-        @pl.when(step + 1 < steps)
-        def _():
-            fetch(step + 1, 1 - slot)
-
-        for i in range(STEP):
+        width = blocks * BW
+        lane = lax.broadcasted_iota(jnp.int32, (1, width), 1) // BW
+        for i in range(blocks):
             index = step * STEP + i
 
             @pl.when(index < total)
@@ -263,34 +262,38 @@
                 xbuf[slot, :, i * BW : (i + 1) * BW] = zero
                 abuf[slot, :, i * BW : (i + 1) * BW] = zero
 
-        x = xbuf[slot]
+        x = xbuf[slot, :, :width]
         inputs = x.astype(BF16)
-        targets = (TARGET_GAIN * (abuf[slot] - x)).astype(BF16)
-        act_one, slope1[...] = activate(dot(w1t[...], inputs))
-        act_two, slope2[...] = activate(dot(w2t[...], act_one))
+        targets = (TARGET_GAIN * (abuf[slot, :, :width] - x)).astype(BF16)
+        act_one, slope1[:, :width] = activate(dot(w1t[...], inputs))
+        act_two, slope2[:, :width] = activate(dot(w2t[...], act_one))
         output = dot(w3t[...], act_two)
-        times = jnp.ones((1, STEP * BW), F32)
-        for i in range(STEP):
+        times = jnp.ones((1, width), F32)
+        for i in range(blocks):
             index = step * STEP + i
             often = jnp.where(index < total, meta[2 + groups + jnp.minimum(index, groups - 1)], 1)
             times = jnp.where(lane == i, often.astype(F32), times)
         error = ((output - targets.astype(F32)) / count).astype(BF16)
         error = (error.astype(F32) * times).astype(BF16)
         grads[:, :, :, 72:] += dot_t(act_two, error).reshape(2, 8, 8, 8, BW)
-        delta_two = (dot(w3[...], error) * slope2[...]).astype(BF16)
+        delta_two = (dot(w3[...], error) * slope2[:, :width]).astype(BF16)
         for j in range(0, hid // BW, 2):
             both = dot_t(act_one, delta_two[j * BW : (j + 2) * BW])
             for k in (0, 1):
                 at = (j + k) * 8
                 grads[:, :, :, at : at + 8] += both[:, k * BW : (k + 1) * BW].reshape(2, 8, 8, 8, BW)
-        delta_one = (dot(w2[...], delta_two) * slope1[...]).astype(BF16)
+        delta_one = (dot(w2[...], delta_two) * slope1[:, :width]).astype(BF16)
         for j in range(0, hid // BW, 2):
             both = dot_t(inputs, delta_one[j * BW : (j + 2) * BW])
             for k in (0, 1):
                 grads[:, :, j + k, 64:72] += both[:, k * BW : (k + 1) * BW].reshape(2, 8, 8, BW)
-        return carry
 
     lax.fori_loop(0, steps, body, 0)
+
+    @pl.when(steps * STEP < total)
+    def _():
+        learn(steps, STEP // 2)
+
     out = pltpu.make_async_copy(grads.at[core], own, leave)
     out.start()
     store_split(send, grads[1 - core].reshape(SHARDS, 80, BW))

time: 167 us -> 167 us (level)
    all_to_all x1, blocking collectives: 45.7 us -> 48 us  [sum_everywhere(): held = lax.all_to_all(pair.reshape(-1, BW), PLANE, 0, 0, tiled=True)]
where the time goes in v6:
time: 167 us; the launch traced here: 166 us
  blocking collectives  84.9 us (51%)
  Pallas kernels  42.1 us (25%)
  starting transfers between devices  15.1 us (9%)
  other arithmetic  9.42 us (6%)
  local copies, waits for them, and re-layouts  7.26 us (4%)
  waiting for transfers between devices  5.65 us (3%)
  between operations  1.93 us (1%)
    all_to_all x1, blocking collectives, sum_everywhere(): held = lax.all_to_all(pair.reshape(-1, BW), PLANE, 0, 0, tiled=True)  48 us
    all_to_all x1, blocking collectives, sum_everywhere(): sent = lax.all_to_all(sent, PLANE, 0, 0, tiled=True)  21.8 us
    pallas_call x1, Pallas kernels, network(): pl.pallas_call(functools.partial(network_kernel, count), out_shape=(jax.S...  21.1 us
    all_to_all x1, blocking collectives, sum_everywhere(): held = lax.all_to_all(held, RING, 0, 0, tiled=True)  15 us
    ppermute x4, starting transfers between devices, shift(): return lax.ppermute(x, axis, [(i, (i + by) % size) for i in range(size)])  11.5 us
    pallas_call x1, Pallas kernels, stencil_call(): pl.pallas_call(stencil_kernel, out_shape=jax.ShapeDtypeStruct(state.shape...  11.2 us
    pallas_call x1, Pallas kernels, prepare(): pl.pallas_call(prepare_kernel, out_shape=[jax.ShapeDtypeStruct((2 + 2 * g...  7.24 us
    ppermute x1, starting transfers between devices, sum_everywhere(): away = lax.ppermute(sent, 'c', swap)  3.52 us
  transfers between devices with their start and end apart: 6, of which 2 were waited for; matrix products, arithmetic and copies ran while one was open for 5% of the time, Pallas kernels for 4%

profile of v6, /device:TPU:1, one launch (start us, length us, event | category | flops | bytes accessed | tf_op | source)
XLA Modules:
  0.0 166.3 jit_solution(15351045265174315555)
XLA Ops:
  0.6 1.9 %fusion.5 = (f32[128,16,2]{2,1,0:T(8,128)S(1)}, f32[128,16,2]{2,1,0:T(8,128)S(1)}) fusion(f32[128,16,512]{2,1,0:T(8,128)} %state.3), kind=kLoop, calls=%fused_computation.33 | loop fusion | bytes 65536 | tf_op jit(solution)/shard_map/slice | solution.py:80
  3.0 1.4 collective-permute-start.1
  4.8 1.3 collective-permute-start
  6.1 2.8 %convert.47 = f16[128,16,512]{2,1,0:T(8,128)(2,1)S(1)} convert(f32[128,16,512]{2,1,0:T(8,128)} %state.3) | non-fusion elementwise | flops 1048576 | bytes 6291456 | tf_op jit(solution)/shard_map/convert.32
  8.8 0.5 fusion.6
  9.9 2.8 %collective-permute-start.3 = (f16[129,2,512]{2,1,0:T(2,128)(2,1)S(1)}, f16[129,2,512]{2,1,0:T(2,128)(2,1)S(1)}, u32[]{:S(2)}, u32[]{:S(2)}) collective-permute-start(f16[129,2,512]{2,1,0:T(2,128)(2,1)S(1)} %pad_maximum_fusion.2), channel_id=1, source_target_pairs={{0,4},{4,8},{8,12},{12,16},{16,20},{20,24},{24,28},{28,32},{32,36}... | collective-permute-start | bytes 792584 | tf_op jit(solution)/shard_map/ppermute | solution.py:29
  13.1 6.0 %collective-permute-start.2 = (f16[129,2,512]{2,1,0:T(2,128)(2,1)S(1)}, f16[129,2,512]{2,1,0:T(2,128)(2,1)S(1)}, u32[]{:S(2)}, u32[]{:S(2)}) collective-permute-start(f16[129,2,512]{2,1,0:T(2,128)(2,1)S(1)} %pad_maximum_fusion.1), channel_id=1, source_target_pairs={{0,124},{4,0},{8,4},{12,8},{16,12},{20,16},{24,20},{28,24},{32,28}... | collective-permute-start | bytes 792584 | tf_op jit(solution)/shard_map/ppermute | solution.py:29
  19.1 0.6 pad_add_fusion.where
  19.7 0.6 reduce.1.tiles
  20.3 7.2 %prepare.1 = (s32[66]{0:T(128)}, bf16[1024,128]{1,0:T(8,128)(2,1)}, bf16[1024,1024]{1,0:T(8,128)(2,1)}, bf16[1024,1024]{1,0:T(8,128)(2,1)}, bf16[128,1024]{1,0:T(8,128)(2,1)}, /*index=5*/bf16[1024,128]{1,0:T(8,128)(2,1)}) custom-call(s32[2]{0:T(128)} %pad_add_fusion.where, s32[384]{0:T(512)} %reduce.1.tiles, s32[384]{0:T(512)} %places.1, ...), custom_call_target="tpu_custom_call" | custom-call | flops 20000000 | bytes 9000000 | tf_op jit(solution)/shard_map/prepare/pallas_call | solution.py:189
  28.1 0.5 copy.17
  28.6 1.3 maximum_bitcast_fusion.edge_cols
  30.4 0.6 pad_maximum_fusion.4.tips
  31.2 11.2 %stencil.1.after = f32[128,16,512]{2,1,0:T(8,128)} custom-call(f32[128]{0:T(128)} %diffusion.1, f32[4,128]{1,0:T(4,128)} %pad_maximum_fusion.4.tips, f32[128,16,512]{2,1,0:T(8,128)} %state.3, f32[129,2,512]{2,1,0:T(2,128)} %copy-done.5, f32[129,2,512]{2,1,0:T(2,128)} %copy-done.4, f32[128,16,128]{2,1,0:T(8,128)} %maximum_bitcast_fusion.edge_cols), custom_call_target="tpu_custom_call" | custom-call | tf_op jit(solution)/shard_map/stencil/pallas_call | solution.py:112
  42.4 21.1 %network.1 = (f32[8,8,80,128]{3,2,1,0:T(8,128)}, bf16[64,88,128]{2,1,0:T(8,128)(2,1)}) custom-call(s32[66]{0:T(128)} %get-tuple-element.15.meta, f32[128,16,512]{2,1,0:T(8,128)} %state.3, f32[128,16,512]{2,1,0:T(8,128)} %stencil.1.after, bf16[1024,128]{1,0:T(8,128)(2,1)} %get-tuple-element.16.refs_0_, bf16[1024,1024]{1,0:T(8,128)(2,1)} %get-tuple-element.17.refs_1_, ...), custom_call_target="tpu_custom_call" | custom-call | tf_op jit(solution)/shard_map/network/pallas_call | solution.py:308
  63.6 3.4 %collective-permute-done.4 = bf16[64,88,128]{2,1,0:T(8,128)(2,1)S(1)} collective-permute-done((bf16[64,88,128]{2,1,0:T(8,128)(2,1)}, bf16[64,88,128]{2,1,0:T(8,128)(2,1)S(1)}, u32[]{:S(2)}, u32[]{:S(2)}) %collective-permute-start.4) | collective-permute-done | bytes 1441824 | tf_op jit(solution)/shard_map/ppermute | solution.py:390
  67.9 48.0 %all_to_all.21 = bf16[16,352,128]{2,1,0:T(8,128)(2,1)S(1)} all-to-all(bf16[16,352,128]{2,1,0:T(8,128)(2,1)S(1)} %bitcast.34), channel_id=1, replica_groups=mesh['z'=4,'y'=4,'xh'=2,'xl'=2,'c'=2] {'z','y'}, dimensions={0} | all-to-all | bytes 2883584 | tf_op jit(solution)/shard_map/all_to_all | solution.py:396
  116.2 15.0 %all_to_all.22 = f32[4,320,128]{2,1,0:T(8,128)S(1)} all-to-all(f32[4,320,128]{2,1,0:T(8,128)S(1)} %broadcast_in_dim.25), channel_id=1, replica_groups=mesh['z'=4,'y'=4,'xh'=2,'xl'=2,'c'=2] {'xh','xl'}, dimensions={0} | all-to-all | bytes 1310720 | tf_op jit(solution)/shard_map/all_to_all | solution.py:402
  131.3 0.6 abs_reduce_fusion
  132.9 21.8 %all_to_all.23 = f16[16,328,128]{2,1,0:T(8,128)(2,1)S(1)} all-to-all(f16[16,328,128]{2,1,0:T(8,128)(2,1)S(1)} %broadcast_in_dim.26), channel_id=1, replica_groups=mesh['z'=4,'y'=4,'xh'=2,'xl'=2,'c'=2] {'z','y'}, dimensions={0} | all-to-all | bytes 2686976 | tf_op jit(solution)/shard_map/all_to_all | solution.py:408
  154.7 3.5 %collective-permute-start.5 = (f16[5248,128]{1,0:T(8,128)(2,1)S(1)}, f16[5248,128]{1,0:T(8,128)(2,1)S(1)}, u32[]{:S(2)}, u32[]{:S(2)}) collective-permute-start(f16[5248,128]{1,0:T(8,128)(2,1)S(1)} %bitcast.35), channel_id=1, source_target_pairs={{0,1},{1,0},{2,3},{3,2},{4,5},{5,4},{6,7},{7,6},{8,9},{9,8},{10,11... | collective-permute-start | bytes 4030472 | tf_op jit(solution)/shard_map/ppermute | solution.py:409
  158.7 2.2 %collective-permute-done.5 = f16[5248,128]{1,0:T(8,128)(2,1)S(1)} collective-permute-done((f16[5248,128]{1,0:T(8,128)(2,1)S(1)}, f16[5248,128]{1,0:T(8,128)(2,1)S(1)}, u32[]{:S(2)}, u32[]{:S(2)}) %collective-permute-start.5) | collective-permute-done | bytes 1343520 | tf_op jit(solution)/shard_map/ppermute | solution.py:409
  161.5 1.9 %copy-done = f32[1024,1024]{1,0:T(8,128)S(1)} copy-done((f32[1024,1024]{1,0:T(8,128)S(1)}, f32[1024,1024]{1,0:T(8,128)}, u32[]{:S(2)}) %copy-start) | copy-done | bytes 4194328
  163.6 2.6 %update.1 = (f32[128,1024]{1,0:T(8,128)}, f32[1024,1024]{1,0:T(8,128)}, f32[1024,128]{1,0:T(8,128)}) custom-call(s32[1]{0:T(128)} %bitcast.11.core, f32[8,8,80,128]{3,2,1,0:T(8,128)S(1)} %bitcast.32, f32[8,8,80,128]{3,2,1,0:T(8,128)S(1)} %bitcast.33, f32[128,1024]{1,0:T(8,128)S(1)} %copy-done.1, f32[1024,1024]{1,0:T(8,128)S(1)} %copy-done, ...), custom_call_target="tpu_custom_call" | custom-call | tf_op jit(solution)/shard_map/update/pallas_call | solution.py:373
  (59 shorter events, 5.4 us)
Async XLA Ops:
  3.0 6.4 %collective-permute-start.1 = (f32[2,16,128]{2,1,0:T(8,128)S(1)}, f32[2,16,128]{2,1,0:T(8,128)S(1)}, u32[]{:S(2)}, u32[]{:S(2)}) collective-permute-start(f32[2,16,128]{2,1,0:T(8,128)S(1)} %bitcast.43), channel_id=1, source_target_pairs={{0,3},{1,0},{2,1},{3,2},{4,7},{5,4},{6,5},{7,6},{8,11},{9,8},{10,9... | collective-permute-start | bytes 49160 | tf_op jit(solution)/shard_map/ppermute | solution.py:29
  4.8 14.9 %copy-start.6 = (s32[384,1]{0,1:T(1,128)S(1)}, s32[384,1]{0,1:T(1,128)}, u32[]{:S(2)}) copy-start(s32[384,1]{0,1:T(1,128)} %param.12) | copy-start | bytes 4612
  4.8 4.6 %collective-permute-start = (f32[2,16,128]{2,1,0:T(8,128)S(1)}, f32[2,16,128]{2,1,0:T(8,128)S(1)}, u32[]{:S(2)}, u32[]{:S(2)}) collective-permute-start(f32[2,16,128]{2,1,0:T(8,128)S(1)} %bitcast.42), channel_id=1, source_target_pairs={{0,1},{1,2},{2,3},{3,0},{4,5},{5,6},{6,7},{7,4},{8,9},{9,10},{10,1... | collective-permute-start | bytes 49160 | tf_op jit(solution)/shard_map/ppermute | solution.py:29
  9.9 20.0 %collective-permute-start.3 = (f16[129,2,512]{2,1,0:T(2,128)(2,1)S(1)}, f16[129,2,512]{2,1,0:T(2,128)(2,1)S(1)}, u32[]{:S(2)}, u32[]{:S(2)}) collective-permute-start(f16[129,2,512]{2,1,0:T(2,128)(2,1)S(1)} %pad_maximum_fusion.2), channel_id=1, source_target_pairs={{0,4},{4,8},{8,12},{12,16},{16,20},{20,24},{24,28},{28,32},{32,36}... | collective-permute-start | bytes 792584 | tf_op jit(solution)/shard_map/ppermute | solution.py:29
  13.1 17.1 %collective-permute-start.2 = (f16[129,2,512]{2,1,0:T(2,128)(2,1)S(1)}, f16[129,2,512]{2,1,0:T(2,128)(2,1)S(1)}, u32[]{:S(2)}, u32[]{:S(2)}) collective-permute-start(f16[129,2,512]{2,1,0:T(2,128)(2,1)S(1)} %pad_maximum_fusion.1), channel_id=1, source_target_pairs={{0,124},{4,0},{8,4},{12,8},{16,12},{20,16},{24,20},{28,24},{32,28}... | collective-permute-start | bytes 792584 | tf_op jit(solution)/shard_map/ppermute | solution.py:29
  30.1 0.9 copy-start.4
  30.4 0.8 copy-start.5
  63.5 3.7 %copy-start.3 = (f32[8,8,80,128]{3,2,1,0:T(8,128)S(1)}, f32[8,8,80,128]{3,2,1,0:T(8,128)}, u32[]{:S(2)}) copy-start(f32[8,8,80,128]{3,2,1,0:T(8,128)} %get-tuple-element.21) | copy-start | bytes 7864324
  63.5 3.5 %collective-permute-start.4 = (bf16[64,88,128]{2,1,0:T(8,128)(2,1)}, bf16[64,88,128]{2,1,0:T(8,128)(2,1)S(1)}, u32[]{:S(2)}, u32[]{:S(2)}) collective-permute-start(bf16[64,88,128]{2,1,0:T(8,128)(2,1)} %get-tuple-element.22), channel_id=1, source_target_pairs={{0,1},{1,0},{2,3},{3,2},{4,5},{5,4},{6,7},{7,6},{8,9},{9,8},{10,11... | collective-permute-start | bytes 4325384 | tf_op jit(solution)/shard_map/ppermute | solution.py:390
  154.7 6.2 %collective-permute-start.5 = (f16[5248,128]{1,0:T(8,128)(2,1)S(1)}, f16[5248,128]{1,0:T(8,128)(2,1)S(1)}, u32[]{:S(2)}, u32[]{:S(2)}) collective-permute-start(f16[5248,128]{1,0:T(8,128)(2,1)S(1)} %bitcast.35), channel_id=1, source_target_pairs={{0,1},{1,0},{2,3},{3,2},{4,5},{5,4},{6,7},{7,6},{8,9},{9,8},{10,11... | collective-permute-start | bytes 4030472 | tf_op jit(solution)/shard_map/ppermute | solution.py:409
  161.1 2.2 %copy-start = (f32[1024,1024]{1,0:T(8,128)S(1)}, f32[1024,1024]{1,0:T(8,128)}, u32[]{:S(2)}) copy-start(f32[1024,1024]{1,0:T(8,128)} %refs_1_.1) | copy-start | bytes 12582916
  161.2 2.3 %copy-start.1 = (f32[128,1024]{1,0:T(8,128)S(1)}, f32[128,1024]{1,0:T(8,128)}, u32[]{:S(2)}) copy-start(f32[128,1024]{1,0:T(8,128)} %refs_0_.1) | copy-start | bytes 1572868
  161.2 2.4 %copy-start.2 = (f32[1024,128]{1,0:T(8,128)S(1)}, f32[1024,128]{1,0:T(8,128)}, u32[]{:S(2)}) copy-start(f32[1024,128]{1,0:T(8,128)} %refs_2_.1) | copy-start | bytes 1572868
